TPU v7x, 32 devices: a whole 2x2x4 slice. The times are simulated.
32 devices in a mesh: member: 2 (over y), lon: 8 (over z, x), lat: 2 (over core).
Axes of the slice: x: 2, y: 2, z: 4, core: 2. Of those that a mesh axis runs over, the one named last changes fastest.
Arguments:
- state_tokens: bfloat16 [8, 24, 96, 768], P('member', 'lat', 'lon'), parts along dimension 0, may hold values from -32 to 32
- land_mask: int32 [24, 96], P('lat', 'lon'), may hold values 0 or 1
- pad_mask: int32 [24], replicated, may hold values from 0 to 1, as said below
- land_embed: float32 [2, 768], replicated, may hold values from -3 to 3
- w_qkv: bfloat16 [768, 1152], replicated, may hold values from -0.21875 to 0.21875
- w_proj: bfloat16 [384, 768], replicated, may hold values from -0.3125 to 0.3125
- proj_bias: float32 [768], replicated, may hold values from -4 to 4
- norm_gain: float32 [768], replicated, may hold values from 0.5 to 1.5
- norm_shift: float32 [768], replicated, may hold values from -1.5 to 1.5
- bias_table: bfloat16 [4, 2, 12, 3312], P('lat'), may hold values from -3.5 to 320
- index_table: int32 [144, 144], replicated, may hold values from 0 to 3311
Outputs:
- result: bfloat16 [8, 24, 96, 768], P('member', 'lat', 'lon'), parts along dimension 0
There are 2 independent parts, one for each index of `member`. A program takes and returns all parts, laid end to end along the dimension named above; an argument that names none is the same for every part. Nothing has to cross between parts.
Inputs may be any that keep to these rules, and one draw needn't show every extreme that they name: pad_mask is 1 on every row except at most the first 2 and the last 2 of the 24 rows, which are 0 where padded; one of the two ends has exactly 2 padding rows.
All inputs are finite; a program needn't handle non-finite values. No bound on the sum of `land_mask` on one device may be relied on, other than what follows from the above.
Results may differ from a plain program's by a relative error of at most 0.0085.
Values may be sent and summed in bfloat16 or wider, within the bound.
A program may use at most 64 MiB of HBM per device.

v0:
```python
import jax
import jax.numpy as jnp
from jax import lax
from jax.sharding import PartitionSpec as P

HEADS = 12
HEAD_DIM = 32
WIN_Z = 2
WIN_LAT = 6
WIN_LON = 12
WIN_TOK = 144


norm_epsilon = 1e-05


def from_behind(shard, axis, by):
    size = lax.axis_size(axis)
    return lax.ppermute(shard, axis, [(i, (i + by) % size) for i in range(size)])


def as_sent(shard):

    def short(part):
        return part.astype(jnp.bfloat16) if part.dtype == jnp.float32 else part

    return jax.tree.map(short, shard)


def region_of(position, length, window):
    half_window = window // 2
    return jnp.where(
        position < length - window, 0, jnp.where(position < length - half_window, 1, 2)
    ).astype(jnp.int32)


def window_rules(levels, lat_start, lat_rows, lat_total, pad_mask):
    tokens = jnp.arange(WIN_TOK, dtype=jnp.int32)
    level_offset = tokens // (WIN_LAT * WIN_LON)
    row_offset = tokens // WIN_LON % WIN_LAT
    level_index = (
        jnp.arange(levels // WIN_Z, dtype=jnp.int32)[:, None] * WIN_Z + level_offset[None, :]
    )
    row_index = (
        lat_start
        + jnp.arange(lat_rows // WIN_LAT, dtype=jnp.int32)[:, None] * WIN_LAT
        + row_offset[None, :]
    )
    region = (
        region_of(level_index, levels, WIN_Z)[:, None, :] * 3
        + region_of(row_index, lat_total, WIN_LAT)[None, :, :]
    )
    source_row = (row_index + WIN_LAT // 2) % lat_total
    lookup = (
        source_row[:, :, None] == jnp.arange(lat_total, dtype=jnp.int32)[None, None, :]
    ).astype(jnp.int32)
    usable = jnp.sum(lookup * pad_mask[None, None, :], axis=-1) == 1
    return (region[:, :, :, None] == region[:, :, None, :]) & usable[None, :, None, :]


def earth_bias(bias_table, index_table):
    lat_windows, z_windows, heads, positions = bias_table.shape
    table_rows = bias_table.reshape(lat_windows * z_windows * heads, positions).T
    picked = jnp.take(table_rows, index_table.reshape(-1), axis=0)
    picked = picked.reshape(WIN_TOK, WIN_TOK, lat_windows, z_windows, heads).astype(jnp.float32)
    return jnp.transpose(picked, (3, 2, 4, 0, 1))


def to_windows(layout):
    levels, lat_rows, lon_columns, channels = layout.shape
    shaped = layout.reshape(
        levels // WIN_Z,
        WIN_Z,
        lat_rows // WIN_LAT,
        WIN_LAT,
        lon_columns // WIN_LON,
        WIN_LON,
        channels,
    )
    shaped = shaped.transpose(0, 2, 4, 1, 3, 5, 6)
    return shaped.reshape(
        levels // WIN_Z, lat_rows // WIN_LAT, lon_columns // WIN_LON, WIN_TOK, channels
    )


def from_windows(window_tiles):
    z_windows, lat_windows, lon_windows, tokens, channels = window_tiles.shape
    shaped = window_tiles.reshape(
        z_windows, lat_windows, lon_windows, WIN_Z, WIN_LAT, WIN_LON, channels
    )
    shaped = shaped.transpose(0, 3, 1, 4, 2, 5, 6)
    return shaped.reshape(z_windows * WIN_Z, lat_windows * WIN_LAT, lon_windows * WIN_LON, channels)


def attend(windows, bias_full, allowed):
    pieces = windows.reshape(windows.shape[:-1] + (3, HEADS, HEAD_DIM))
    queries = pieces[..., 0, :, :]
    key_rows = pieces[..., 1, :, :]
    value_rows = pieces[..., 2, :, :]
    scores = jnp.einsum(
        "abcthd,abcuhd->abchtu", queries, key_rows, preferred_element_type=jnp.float32
    )
    scores = scores / jnp.sqrt(jnp.float32(HEAD_DIM)) + bias_full[:, :, None]
    scores = jnp.where(allowed[:, :, None, None], scores, -jnp.inf)
    largest = jnp.max(scores, axis=-1, keepdims=True)
    powers = jnp.exp(scores - largest)
    weights = (powers / jnp.sum(powers, axis=-1, keepdims=True)).astype(jnp.bfloat16)
    attended = jnp.einsum(
        "abchtu,abcuhd->abcthd", weights, value_rows, preferred_element_type=jnp.float32
    ).astype(jnp.bfloat16)
    return attended.reshape(attended.shape[:4] + (HEADS * HEAD_DIM,))


def finish(attended, w_proj, proj_bias, norm_gain, norm_shift):
    projected = jnp.dot(attended, w_proj, preferred_element_type=jnp.float32) + proj_bias
    average = jnp.mean(projected, axis=-1, keepdims=True)
    centered = projected - average
    spread = jnp.mean(centered * centered, axis=-1, keepdims=True)
    return centered * lax.rsqrt(spread + norm_epsilon) * norm_gain + norm_shift


def on_device(
    state_tokens,
    land_mask,
    pad_mask,
    land_embed,
    w_qkv,
    w_proj,
    proj_bias,
    norm_gain,
    norm_shift,
    bias_table,
    index_table,
):
    levels, lat_rows, lon_columns, features = state_tokens.shape
    lat_total = lat_rows * lax.axis_size("lat")
    lat_start = lax.axis_index("lat") * lat_rows
    level_half = WIN_Z // 2
    lat_half = WIN_LAT // 2
    lon_half = WIN_LON // 2
    embedded = jnp.where(land_mask[:, :, None] == 1, land_embed[1], land_embed[0])
    hidden = (state_tokens.astype(jnp.float32) + embedded[None]).astype(jnp.bfloat16)
    own_rows = jnp.dot(hidden, w_qkv, preferred_element_type=jnp.float32).astype(jnp.bfloat16)
    rolled = jnp.roll(own_rows, -level_half, axis=0)
    incoming = from_behind(rolled[:, :, :lon_half], "lon", -1)
    rolled = jnp.concatenate([rolled[:, :, lon_half:], incoming], axis=2)
    incoming = from_behind(rolled[:, :lat_half], "lat", -1)
    projections = jnp.concatenate([rolled[:, lat_half:], incoming], axis=1)
    bias_full = earth_bias(bias_table, index_table)
    allowed = window_rules(levels, lat_start, lat_rows, lat_total, pad_mask)
    attended = from_windows(attend(to_windows(projections), bias_full, allowed))
    normed = finish(attended, w_proj, proj_bias, norm_gain, norm_shift)
    incoming = from_behind(normed[:, -lat_half:].astype(jnp.bfloat16), "lat", 1).astype(jnp.float32)
    normed = jnp.concatenate([incoming, normed[:, :-lat_half]], axis=1)
    incoming = from_behind(as_sent(normed[:, :, -lon_half:]), "lon", 1)
    normed = jnp.concatenate([incoming, normed[:, :, :-lon_half]], axis=2)
    normed = jnp.roll(normed, level_half, axis=0)
    return (hidden.astype(jnp.float32) + normed).astype(jnp.bfloat16)


def solution(mesh):
    in_specs = (
        P("member", "lat", "lon", None),
        P("lat", "lon"),
        P(),
        P(),
        P(),
        P(),
        P(),
        P(),
        P(),
        P("lat", None, None, None),
        P(),
    )
    out_specs = P("member", "lat", "lon", None)
    return jax.shard_map(
        on_device, mesh=mesh, in_specs=in_specs, out_specs=out_specs, check_vma=False
    )
```

profile of v0, /device:TPU:0, one launch (start us, length us, event | category | flops | bytes accessed | tf_op | source)
XLA Modules:
  0.0 160.7 jit_solution(6752801541054168498)
XLA Ops:
  0.0 0.9 slice_reduce_fusion.1
  0.9 0.7 broadcast_compare_fusion
  1.6 0.1 broadcast_select_fusion.2
  1.7 0.8 copy-done.2
  2.5 2.9 %convolution_convert_fusion = bf16[4,12,12,1152]{3,2,1,0:T(8,128)(2,1)S(1)} fusion(bf16[768,1152]{1,0:T(8,128)(2,1)S(1)} %copy-done, bf16[4,12,12,768]{3,0,2,1:T(4,128)(2,1)} %param.11, f32[12,12,768]{2,1,0:T(8,128)S(1)} %broadcast_select_fusion.2), kind=kOutput, calls=%fused_computation.12 | convolution fusion | flops 1021206528 | bytes 4423680 | tf_op jit(solution)/shard_map/dot_general | solution.py:143
  5.4 0.1 slice.76
  5.6 0.4 fusion.18
  6.0 0.3 copy.66
  6.3 6.2 %collective-permute-start = (bf16[4,12,6,1152]{3,0,2,1:T(4,128)(2,1)S(1)}, bf16[4,12,6,1152]{3,0,2,1:T(4,128)(2,1)S(1)}, u32[]{:S(2)}, u32[]{:S(2)}) collective-permute-start(bf16[4,12,6,1152]{3,0,2,1:T(4,128)(2,1)S(1)} %copy.66), channel_id=1, source_target_pairs={{0,14},{2,0},{4,2},{6,4},{8,6},{10,8},{12,10},{14,12},{1,15},{3,1}... | collective-permute-start | bytes 1990664 | tf_op jit(solution)/shard_map/ppermute | solution.py:19
  12.8 0.2 reshape.255
  13.1 0.3 fusion.33
  13.4 13.4 %collective-permute-done = bf16[4,12,6,1152]{3,0,2,1:T(4,128)(2,1)S(1)} collective-permute-done((bf16[4,12,6,1152]{3,0,2,1:T(4,128)(2,1)S(1)}, bf16[4,12,6,1152]{3,0,2,1:T(4,128)(2,1)S(1)}, u32[]{:S(2)}, u32[]{:S(2)}) %collective-permute-start) | collective-permute-done | bytes 663584 | tf_op jit(solution)/shard_map/ppermute | solution.py:19
  26.7 0.1 copy.67
  26.8 0.9 pad_maximum_fusion.6
  27.8 0.8 compare_and_fusion
  28.6 1.0 copy.73
  29.7 0.1 reshape.254
  29.8 0.4 copy.74
  30.2 42.0 %gather_fusion = bf16[20736,48]{1,0:T(8,128)(2,1)} fusion(bf16[3312,48]{1,0:T(8,128)(2,1)S(1)} %bitcast.64, s32[21504]{0:T(1024)S(1)} %pad_clamp_fusion), kind=kCustom, calls=%fused_computation | custom fusion | bytes 4064256 | tf_op jit(solution)/shard_map/jit(_take)/gather | solution.py:64
  72.2 6.0 %copy.75 = bf16[20736,48]{0,1:T(8,128)(2,1)} copy(bf16[20736,48]{1,0:T(8,128)(2,1)} %gather_fusion) | data formatting | bytes 3981312 | tf_op jit(solution)/shard_map/jit(_take)/gather | solution.py:64
  78.2 8.2 %gather.7 = bf16[144,144,2,2,12]{1,0,4,3,2:T(8,128)(2,1)} reshape(bf16[20736,48]{0,1:T(8,128)(2,1)} %copy.75) | data formatting | bytes 3981312 | tf_op jit(solution)/shard_map/jit(_take)/gather | solution.py:64
  86.4 6.2 %copy.76 = bf16[144,144,2,2,12]{0,1,4,2,3:T(8,128)(2,1)} copy(bf16[144,144,2,2,12]{1,0,4,3,2:T(8,128)(2,1)} %gather.7) | data formatting | bytes 3981312 | tf_op jit(solution)/shard_map/jit(_take)/gather | solution.py:64
  92.6 0.1 copy.72
  92.8 0.4 fusion.14
  93.2 0.3 pad_maximum_fusion.4
  93.5 1.0 copy.98
  94.6 6.7 %reshape_reshape.6 = bf16[2,2,1,144,3,12,32]{6,5,4,1,3,0,2:T(8,128)(2,1)} reshape(bf16[2,2,1,2,6,12,1152]{6,1,5,4,3,0,2:T(2,128)(2,1)S(1)} %bitcast.66) | data formatting | bytes 2654208 | tf_op jit(solution)/shard_map/reshape;reshape | solution.py:96
  101.3 6.7 %fusion.45 = (bf16[2,2,1,144,1,12,32]{6,5,4,1,3,0,2:T(8,128)(2,1)}, bf16[2,2,1,144,1,12,32]{6,5,4,1,3,0,2:T(8,128)(2,1)}, bf16[2,2,1,144,1,12,32]{6,5,4,1,3,0,2:T(8,128)(2,1)}) fusion(bf16[2,2,1,144,3,12,32]{6,5,4,1,3,0,2:T(8,128)(2,1)} %reshape_reshape.6), kind=kLoop, calls=%fused_computation.89 | loop fusion | bytes 2654208 | tf_op jit(solution)/shard_map/slice | solution.py:99
  107.9 3.3 %copy.90 = bf16[2,2,1,144,1,12,32]{3,6,5,1,0,4,2:T(8,128)(2,1)S(1)} copy(bf16[2,2,1,144,1,12,32]{6,5,4,1,3,0,2:T(8,128)(2,1)} %get-tuple-element.8) | data formatting | bytes 884736
  111.3 3.4 %copy.91 = bf16[2,2,1,144,1,12,32]{3,6,5,1,0,4,2:T(8,128)(2,1)S(1)} copy(bf16[2,2,1,144,1,12,32]{6,5,4,1,3,0,2:T(8,128)(2,1)} %get-tuple-element.9) | data formatting | bytes 884736
  114.7 3.6 %copy.89 = bf16[2,2,1,144,1,12,32]{3,6,5,1,0,4,2:T(8,128)(2,1)S(1)} copy(bf16[2,2,1,144,1,12,32]{6,5,4,1,3,0,2:T(8,128)(2,1)} %get-tuple-element.7) | data formatting | bytes 884736
  118.3 8.1 %fusion.46 = (f32[2,2,12,144]{3,2,1,0:T(8,128)S(1)}, f32[2,2,12,144,144]{3,4,2,1,0:T(8,128)}) fusion(pred[2,2,144,144]{2,3,1,0:T(8,128)(4,1)S(1)} %copy-done.7, bf16[144,144,2,2,12]{0,1,4,2,3:T(8,128)(2,1)} %copy.76, pred[144,144]{0,1:T(8,128)(4,1)S(1)} %copy.72, bf16[2,2,1,144,1,12,32]{3,6,5,1,0,4,2:T(8,128)(2,1)S(1)} %copy.91, ...), kind=kOutput, calls=%fused_computation.90 | convolution fusion | flops 70668432 | bytes 6988032 | tf_op jit(solution)/shard_map/sub | solution.py:106
  126.4 3.6 %fusion.15 = bf16[2,2,1,144,12,32]{3,5,4,1,0,2:T(8,128)(2,1)S(1)} fusion(f32[2,2,12,144,144]{3,4,2,1,0:T(8,128)} %get-tuple-element.15, f32[2,2,12,144]{3,2,1,0:T(8,128)S(1)} %get-tuple-element.14, bf16[2,2,1,144,1,12,32]{3,6,5,1,0,4,2:T(8,128)(2,1)S(1)} %copy.89), kind=kOutput, calls=%fused_computation.36 | convolution fusion | flops 65912832 | bytes 4893696 | tf_op jit(solution)/shard_map/abchtu,abcuhd->abcthd/dot_general | solution.py:108
  130.0 4.2 %copy.78 = bf16[2,2,1,144,12,32]{5,4,1,3,0,2:T(8,128)(2,1)} copy(bf16[2,2,1,144,12,32]{3,5,4,1,0,2:T(8,128)(2,1)S(1)} %fusion.15) | data formatting | bytes 884736 | tf_op jit(solution)/shard_map/convert_element_type | solution.py:110
  134.2 3.7 %reshape_reshape.7 = bf16[2,2,1,2,6,12,384]{6,1,5,4,3,0,2:T(2,128)(2,1)S(1)} reshape(bf16[2,2,1,144,12,32]{5,4,1,3,0,2:T(8,128)(2,1)} %copy.78) | data formatting | bytes 884736 | tf_op jit(solution)/shard_map/reshape;reshape | solution.py:88
  138.0 0.8 add_reduce_fusion
  138.9 0.5 multiply_reduce_fusion
  139.4 0.5 multiply_add_fusion
  140.0 0.6 collective-permute-start.2
  140.5 0.1 slice.86
  140.7 1.1 collective-permute-done.2
  141.8 0.2 fusion.17
  142.0 0.3 copy.81
  142.4 0.4 collective-permute-start.3
  142.7 15.5 %collective-permute-done.3 = bf16[4,12,6,768]{3,0,2,1:T(4,128)(2,1)S(1)} collective-permute-done((bf16[4,12,6,768]{3,0,2,1:T(4,128)(2,1)S(1)}, bf16[4,12,6,768]{3,0,2,1:T(4,128)(2,1)S(1)}, u32[]{:S(2)}, u32[]{:S(2)}) %collective-permute-start.3) | collective-permute-done | bytes 442400 | tf_op jit(solution)/shard_map/ppermute | solution.py:19
  158.3 0.1 copy_convert_fusion
  158.4 0.6 fusion.10
  159.1 1.6 copy.83
  (41 shorter events, 0.6 us)
Async XLA Ops:
  0.0 2.5 %copy-start = (bf16[768,1152]{1,0:T(8,128)(2,1)S(1)}, bf16[768,1152]{1,0:T(8,128)(2,1)}, u32[]{:S(2)}) copy-start(bf16[768,1152]{1,0:T(8,128)(2,1)} %param.15) | copy-start | bytes 5308420
  1.7 0.8 copy-start.2
  5.6 7.1 %copy-start.11 = (s32[24]{0:T(128)S(1)}, s32[24]{0:T(128)}, u32[]{:S(2)}) copy-start(s32[24]{0:T(128)} %param.13) | copy-start | bytes 292
  5.6 7.2 %copy-start.5 = (s32[144,144]{1,0:T(8,128)S(1)}, s32[144,144]{1,0:T(8,128)}, u32[]{:S(2)}) copy-start(s32[144,144]{1,0:T(8,128)} %param.21) | copy-start | bytes 248836
  6.3 20.4 %collective-permute-start = (bf16[4,12,6,1152]{3,0,2,1:T(4,128)(2,1)S(1)}, bf16[4,12,6,1152]{3,0,2,1:T(4,128)(2,1)S(1)}, u32[]{:S(2)}, u32[]{:S(2)}) collective-permute-start(bf16[4,12,6,1152]{3,0,2,1:T(4,128)(2,1)S(1)} %copy.66), channel_id=1, source_target_pairs={{0,14},{2,0},{4,2},{6,4},{8,6},{10,8},{12,10},{14,12},{1,15},{3,1}... | collective-permute-start | bytes 1990664 | tf_op jit(solution)/shard_map/ppermute | solution.py:19
  27.8 65.4 %collective-permute-start.1 = (bf16[4,3,12,1152]{3,2,1,0:T(8,128)(2,1)}, bf16[4,3,12,1152]{3,2,1,0:T(8,128)(2,1)S(1)}, u32[]{:S(2)}, u32[]{:S(2)}) collective-permute-start(bf16[4,3,12,1152]{3,2,1,0:T(8,128)(2,1)} %pad_maximum_fusion.6), channel_id=1, source_target_pairs={{0,1},{1,0},{2,3},{3,2},{4,5},{5,4},{6,7},{7,6},{8,9},{9,8},{10,11... | collective-permute-start | bytes 995336 | tf_op jit(solution)/shard_map/ppermute | solution.py:19
  114.7 3.6 %copy-start.7 = (pred[2,2,144,144]{2,3,1,0:T(8,128)(4,1)S(1)}, pred[2,2,144,144]{2,3,1,0:T(8,128)(4,1)}, u32[]{:S(2)}) copy-start(pred[2,2,144,144]{2,3,1,0:T(8,128)(4,1)} %compare_and_fusion) | copy-start | bytes 248836
  134.2 3.8 %copy-start.6 = (bf16[384,768]{1,0:T(8,128)(2,1)S(1)}, bf16[384,768]{1,0:T(8,128)(2,1)}, u32[]{:S(2)}) copy-start(bf16[384,768]{1,0:T(8,128)(2,1)} %param.16) | copy-start | bytes 1769476
  134.2 3.8 %copy-start.8 = (f32[768]{0:T(1024)S(1)}, f32[768]{0:T(1024)}, u32[]{:S(2)}) copy-start(f32[768]{0:T(1024)} %param.17) | copy-start | bytes 9220
  138.0 1.4 copy-start.9
  138.0 1.4 copy-start.10
  140.0 1.8 %collective-permute-start.2 = (bf16[4,3,12,768]{3,2,1,0:T(8,128)(2,1)S(1)}, bf16[4,3,12,768]{3,2,1,0:T(8,128)(2,1)S(1)}, u32[]{:S(2)}, u32[]{:S(2)}) collective-permute-start(bf16[4,3,12,768]{3,2,1,0:T(8,128)(2,1)S(1)} %slice.112), channel_id=1, source_target_pairs={{0,1},{1,0},{2,3},{3,2},{4,5},{5,4},{6,7},{7,6},{8,9},{9,8},{10,11... | collective-permute-start | bytes 663560 | tf_op jit(solution)/shard_map/ppermute | solution.py:19
  141.8 16.6 %copy-start.3 = (f32[12,12,768]{2,1,0:T(8,128)S(1)}, f32[12,12,768]{2,1,0:T(8,128)}, u32[]{:S(2)}) copy-start(f32[12,12,768]{2,1,0:T(8,128)} %copy-done.2) | copy-start | bytes 1327108
  141.8 16.6 %copy-start.4 = (bf16[4,12,12,768]{3,0,2,1:T(4,128)(2,1)S(1)}, bf16[4,12,12,768]{3,0,2,1:T(4,128)(2,1)}, u32[]{:S(2)}) copy-start(bf16[4,12,12,768]{3,0,2,1:T(4,128)(2,1)} %param.11) | copy-start | bytes 2654212
  142.4 15.9 %collective-permute-start.3 = (bf16[4,12,6,768]{3,0,2,1:T(4,128)(2,1)S(1)}, bf16[4,12,6,768]{3,0,2,1:T(4,128)(2,1)S(1)}, u32[]{:S(2)}, u32[]{:S(2)}) collective-permute-start(bf16[4,12,6,768]{3,0,2,1:T(4,128)(2,1)S(1)} %copy.81), channel_id=1, source_target_pairs={{0,2},{2,4},{4,6},{6,8},{8,10},{10,12},{12,14},{14,0},{1,3},{3,5},... | collective-permute-start | bytes 1327112 | tf_op jit(solution)/shard_map/ppermute | solution.py:19
  158.4 2.3 %copy-start.1 = (bf16[768,1152]{1,0:T(8,128)(2,1)S(1)}, bf16[768,1152]{1,0:T(8,128)(2,1)}, u32[]{:S(2)}) copy-start(bf16[768,1152]{1,0:T(8,128)(2,1)} %param.15) | copy-start | bytes 5308420
where the time goes:
time: 161 us
  local copies, waits for them, and re-layouts  101 us (63%)
  waiting for transfers between devices  30 us (19%)
  matrix products  15.5 us (10%)
  starting transfers between devices  7.21 us (4%)
  other arithmetic  6.19 us (4%)
    gather x4, local copies, waits for them, and re-layouts, earth_bias(): picked = jnp.take(table_rows, index_table.reshape(-1), axis=0)  62.4 us
    ppermute x4, waiting for transfers between devices, from_behind(): lax.ppermute(shard, axis, [(i, (i + by) % size) for i in range(size)])  30 us
    unnamed x28, local copies, waits for them, and re-layouts  12.2 us
    sub x1, matrix products, attend(): powers = jnp.exp(scores - largest)  8.11 us
    ppermute x4, starting transfers between devices, from_behind(): lax.ppermute(shard, axis, [(i, (i + by) % size) for i in range(size)])  7.21 us
    another operation x1, local copies, waits for them, and re-layouts, attend(): pieces = windows.reshape(windows.shape[:-1] + (3, HEADS, HEAD_DIM))  6.7 us
    slice x1, local copies, waits for them, and re-layouts, attend(): value_rows = pieces[..., 2, :, :]  6.66 us
    convert_element_type x1, local copies, waits for them, and re-layouts, attend(): attended = jnp.einsum('abchtu,abcuhd->abcthd', weights, value_rows, prefe...  4.18 us
  transfers between devices with their start and end apart: 4, of which 3 were waited for; matrix products, arithmetic and copies ran while one was open for 41% of the time, Pallas kernels for 0%

commit v1 on v0

v1 whole, which is shorter than its diff:
```python
import jax
import jax.numpy as jnp
import numpy as np
from jax import lax
from jax.experimental import pallas as pl
from jax.experimental.pallas import tpu as pltpu
from jax.sharding import PartitionSpec as P

HEADS = 12
HEAD_DIM = 32
WIN_Z = 2
WIN_LAT = 6
WIN_LON = 12
WIN_TOK = 144
HALF_LAT = WIN_LAT // 2
HALF_LON = WIN_LON // 2
GROUP = WIN_Z * HALF_LAT * HALF_LON
SLOT = 48
LOW = 256
SHUT = -1e30
WIDTH = HEADS * HEAD_DIM

norm_epsilon = 1e-05


def from_behind(shard, axis, by):
    size = lax.axis_size(axis)
    return lax.ppermute(shard, axis, [(i, (i + by) % size) for i in range(size)])


def group_tokens(a, b):
    dz, di, dj = np.meshgrid(
        np.arange(WIN_Z), np.arange(HALF_LAT), np.arange(HALF_LON), indexing="ij"
    )
    return ((dz * WIN_LAT + a * HALF_LAT + di) * WIN_LON + b * HALF_LON + dj).reshape(-1)


def window_orders():
    groups = [group_tokens(a, b) for a in range(2) for b in range(2)]
    queries = np.concatenate(groups)
    keys = np.concatenate([g[:32] for g in groups] + [g[32:] for g in groups])
    return queries, keys


def token_orders(levels, lat_rows, lon_columns):
    quarters = lat_rows // HALF_LAT
    z_windows = levels // WIN_Z
    rows = 2 * quarters * z_windows * SLOT
    placed = np.full((rows,), -1, np.int32)
    plain = np.full((rows,), -1, np.int32)
    row = 0
    for lon_half in range(2):
        for quarter in range(quarters):
            for zw in range(z_windows):
                a, b = 1 - quarter % 2, 1 - lon_half
                t = 0
                for dz in range(WIN_Z):
                    for di in range(HALF_LAT):
                        for dj in range(HALF_LON):
                            z = (zw * WIN_Z + dz + WIN_Z // 2) % levels
                            i = quarter * HALF_LAT + di
                            j = lon_half * HALF_LON + dj
                            natural = (z * lat_rows + i) * 16 + j
                            place = t if t < 32 else t + 4 * (2 * a + b)
                            placed[row + place] = natural
                            plain[row + t] = natural
                            t += 1
                row += SLOT
    return placed, plain


def bias_kernel(meta_ref, table_ref, out_ref):
    highs = table_ref.shape[1] // 48
    half_row = lax.broadcasted_iota(jnp.int32, (8, LOW), 0) < 4
    low_iota = lax.broadcasted_iota(jnp.int32, (LOW, LOW), 0)

    def look_up(a, tile):
        meta = meta_ref[tile]
        hot = jnp.where(low_iota == meta[0:1], 1.0, 0.0).astype(jnp.bfloat16)
        found = jnp.dot(table_ref[a], hot, preferred_element_type=jnp.float32)
        high = jnp.broadcast_to(meta[1:2], (48, LOW))
        total = found[0:48]
        for k in range(1, highs):
            total = jnp.where(high == k, found[k * 48 : (k + 1) * 48], total)
        pieces = []
        for s in range(2):
            first = jnp.broadcast_to(meta[2 + 2 * s : 3 + 2 * s], (8, LOW))
            second = jnp.broadcast_to(meta[3 + 2 * s : 4 + 2 * s], (8, LOW))
            for kind, allowed in enumerate((first, second, jnp.where(half_row, first, second))):
                part = total[(s * 3 + kind) * 8 : (s * 3 + kind) * 8 + 8]
                pieces.append(jnp.where(allowed == 1, part, SHUT))
        return pieces

    for a in range(2):

        def pair(p, carry, a=a):
            pieces = look_up(a, a * 36 + p)
            for s in range(2):
                for kind in range(3):
                    part = pieces[s * 3 + kind]
                    out_ref[a, s, kind, 2 * p, :, 0:128] = part[:, 0:128]
                    out_ref[a, s, kind, 2 * p + 1, :, 0:128] = part[:, 128:256]
            return carry

        lax.fori_loop(0, 36, pair, 0)
        for tile in range(5):
            pieces = look_up(a, 72 + a * 5 + tile)
            for j in range(16):
                q = tile * 16 + j
                if q < 72:
                    for s in range(2):
                        for kind in range(3):
                            out_ref[a, s, kind, q, :, 128:144] = pieces[s * 3 + kind][
                                :, 16 * j : 16 * j + 16
                            ]


def attend_kernel(
    bias_ref,
    q_ref,
    own_ref,
    left_ref,
    right_ref,
    up_ref,
    down_ref,
    hidden_ref,
    restore_ref,
    w_ref,
    vectors_ref,
    out_ref,
    keys_ref,
    attended_ref,
):
    step = pl.program_id(0)

    @pl.when(step == 0)
    def _():
        def column(c, quarter, zw):
            if quarter < 0:
                return up_ref.at[c, zw]
            if quarter > 3:
                return down_ref.at[c, zw]
            if c == 0:
                return left_ref.at[quarter, zw]
            if c == 3:
                return right_ref.at[quarter, zw]
            return own_ref.at[c - 1, quarter, zw]

        for lat in range(3):
            for lon in range(2):
                for zw in range(2):
                    rest = None
                    for a in range(2):
                        for b in range(2):
                            ref = column(2 * lon + b, 2 * lat - 1 + a, zw)
                            n = 32 * (2 * a + b)
                            keys_ref[2 * lat + lon, zw, n : n + 32, :] = ref[0:32, :]
                            tail = ref[32:48, :]
                            rest = tail if rest is None else rest + tail
                    keys_ref[2 * lat + lon, zw, 128:144, :] = rest

    quarter, lon = step // 2, step % 2
    window = 2 * ((quarter + 1) // 2) + lon
    head_mask = jnp.where(
        lax.broadcasted_iota(jnp.int32, (8, 256), 1) // HEAD_DIM
        == lax.broadcasted_iota(jnp.int32, (8, 256), 0),
        1.0,
        0.0,
    )
    gather_rows = jnp.where(
        lax.broadcasted_iota(jnp.int32, (SLOT, 8 * GROUP), 1) // 8
        == lax.broadcasted_iota(jnp.int32, (SLOT, 8 * GROUP), 0),
        1.0,
        0.0,
    ).astype(jnp.bfloat16)
    queries = []
    for zw in range(2):
        q = q_ref[lon, quarter, zw].astype(jnp.float32)
        tail = (q[32:36] + q[36:40]) + (q[40:44] + q[44:48])
        queries.append(jnp.concatenate([q[0:32], tail], axis=0))
    results = []
    for kind in range(3):
        if kind < 2:
            q = queries[kind][:, 0:256]
            key = keys_ref[window, kind, :, 0:256]
            value = keys_ref[window, kind, :, WIDTH : WIDTH + 256]
        else:
            q = jnp.concatenate([queries[0][:, 256:384], queries[1][:, 256:384]], axis=1)
            key = jnp.concatenate(
                [keys_ref[window, 0, :, 256:384], keys_ref[window, 1, :, 256:384]], axis=1
            )
            value = jnp.concatenate(
                [keys_ref[window, 0, :, 640:768], keys_ref[window, 1, :, 640:768]], axis=1
            )
        spread = (q[:, None, :] * head_mask[None]).reshape(8 * GROUP, 256).astype(jnp.bfloat16)
        scores = lax.dot_general(
            spread, key, (((1,), (1,)), ((), ())), preferred_element_type=jnp.float32
        )
        bias = bias_ref[0, 0, kind].reshape(8 * GROUP, 256)[:, 0:WIN_TOK]
        scores = scores * (HEAD_DIM**-0.5) + bias
        powers = jnp.exp(scores - jnp.max(scores, axis=-1, keepdims=True))
        weights = (powers / jnp.sum(powers, axis=-1, keepdims=True)).astype(jnp.bfloat16)
        mixed = jnp.dot(weights, value, preferred_element_type=jnp.float32)
        mixed = (mixed.reshape(GROUP, 8, 256) * head_mask[None]).reshape(8 * GROUP, 256)
        results.append(
            jnp.dot(
                gather_rows, mixed.astype(jnp.bfloat16), preferred_element_type=jnp.float32
            ).astype(jnp.bfloat16)
        )
    for zw in range(2):
        row = ((lon * 4 + quarter) * 2 + zw) * SLOT
        row = pl.multiple_of(row, SLOT)
        attended_ref[pl.ds(row, SLOT), 0:256] = results[zw]
        attended_ref[pl.ds(row, SLOT), 256:384] = results[2][:, zw * 128 : zw * 128 + 128]

    @pl.when(step == pl.num_programs(0) - 1)
    def _():
        chunk = 192
        for n in range(0, hidden_ref.shape[0], chunk):
            natural = jnp.dot(
                restore_ref[n : n + chunk, :],
                attended_ref[...],
                preferred_element_type=jnp.float32,
            ).astype(jnp.bfloat16)
            projected = (
                jnp.dot(natural, w_ref[...], preferred_element_type=jnp.float32)
                + vectors_ref[0:1, :]
            )
            centered = projected - jnp.mean(projected, axis=-1, keepdims=True)
            spread = jnp.mean(centered * centered, axis=-1, keepdims=True)
            normed = (
                centered * lax.rsqrt(spread + norm_epsilon) * vectors_ref[1:2, :]
                + vectors_ref[2:3, :]
            )
            result = (hidden_ref[n : n + chunk, :].astype(jnp.float32) + normed).astype(
                jnp.bfloat16
            )
            result = result.reshape(chunk // 16, 16, result.shape[-1])
            out_ref[n // 16 : (n + chunk) // 16] = result[:, : out_ref.shape[1], :]


def allowed_pairs(lat_index, lat_total, pad_mask):
    queries, keys = window_orders()
    windows = lat_total // WIN_LAT
    q_level, q_half = queries // 72, queries // 12 % 6 // 3
    k_level, k_row = keys // 72, keys // 12 % 6
    base = 2 * lat_index
    edge = jnp.where(jnp.asarray(q_half == 1), base - 1 + windows, base + 1) % windows
    rows = []
    for window in (edge, jnp.zeros_like(edge) + base):
        source = (window[:, None] * WIN_LAT + jnp.asarray(k_row)[None, :] + HALF_LAT) % lat_total
        usable = jnp.zeros(source.shape, jnp.int32)
        for n in range(pad_mask.shape[0]):
            usable = jnp.where(source == n, pad_mask[n], usable)
        same_half = jnp.asarray(q_half[:, None] == (k_row // 3)[None, :])
        same_row = (window[:, None] != windows - 1) | same_half
        for zw in range(2):
            same_level = jnp.asarray((zw == 0) | (q_level[:, None] == k_level[None, :]))
            rows.append(((usable == 1) & same_row & same_level).astype(jnp.int32))
    return rows


def as_tiles(rows):
    main = rows[:, :128].reshape(72, 256)
    rest = jnp.pad(rows[:, 128:].reshape(2, 72, 16), ((0, 0), (0, 8), (0, 0))).reshape(10, 256)
    return jnp.concatenate([main, rest], axis=0)


def bias_inputs(bias_table, index_table, pad_mask, lat_index, lat_total):
    queries, keys = window_orders()
    to_q = jnp.asarray(np.eye(WIN_TOK)[queries], jnp.bfloat16)
    to_k = jnp.asarray(np.eye(WIN_TOK)[keys].T, jnp.bfloat16)

    def reorder(values):
        picked = jnp.dot(to_q, values.astype(jnp.bfloat16), preferred_element_type=jnp.float32)
        picked = jnp.dot(picked.astype(jnp.bfloat16), to_k, preferred_element_type=jnp.float32)
        return picked.astype(jnp.int32)

    rows = [reorder(index_table % LOW), reorder(index_table // LOW)]
    rows += allowed_pairs(lat_index, lat_total, pad_mask)
    meta = jnp.stack([as_tiles(r) for r in rows], axis=1)
    before = from_behind(bias_table[-1], "lat", 1)
    positions = bias_table.shape[-1]
    highs = -(-positions // LOW)

    def kinds(table):
        table = jnp.pad(table, ((0, 0), (0, 0), (0, highs * LOW - positions)))
        last = jnp.concatenate([table[0, 8:], table[1, 8:]], axis=0)
        return jnp.stack([table[0, :8], table[1, :8], last])

    first, second, third = kinds(before), kinds(bias_table[0]), kinds(bias_table[1])
    tables = jnp.stack([jnp.stack([third, second]), jnp.stack([first, second])])
    tables = tables.reshape(2, 48, highs, LOW).transpose(0, 2, 1, 3).reshape(2, highs * 48, LOW)
    return meta, tables


def on_device(
    state_tokens,
    land_mask,
    pad_mask,
    land_embed,
    w_qkv,
    w_proj,
    proj_bias,
    norm_gain,
    norm_shift,
    bias_table,
    index_table,
):
    levels, lat_rows, lon_columns, features = state_tokens.shape
    assert (levels, lat_rows, lon_columns) == (2 * WIN_Z, 2 * WIN_LAT, WIN_LON)
    lat_total = lat_rows * lax.axis_size("lat")
    embedded = jnp.where(land_mask[:, :, None] == 1, land_embed[1], land_embed[0])
    hidden = (state_tokens.astype(jnp.float32) + embedded[None]).astype(jnp.bfloat16)
    hidden = jnp.pad(hidden, ((0, 0), (0, 0), (0, 16 - lon_columns), (0, 0)))
    hidden = hidden.reshape(levels * lat_rows * 16, features)
    rows = hidden.shape[0]
    placed, plain = token_orders(levels, lat_rows, lon_columns)
    natural = jnp.arange(rows, dtype=jnp.int32)
    to_groups = (jnp.asarray(placed)[:, None] == natural[None, :]).astype(jnp.bfloat16)
    restore = (natural[:, None] == jnp.asarray(plain)[None, :]).astype(jnp.bfloat16)
    grouped = jnp.dot(to_groups, hidden, preferred_element_type=jnp.float32).astype(jnp.bfloat16)
    shape = (2, 4, 2, SLOT)
    kv = jnp.dot(grouped, w_qkv[:, WIDTH:], preferred_element_type=jnp.float32)
    kv = kv.astype(jnp.bfloat16).reshape(shape + (2 * WIDTH,))
    right = from_behind(kv[0], "lon", -1)
    left = from_behind(kv[1], "lon", 1)
    up = from_behind(jnp.stack([left[3], kv[0, 3], kv[1, 3], right[3]]), "lat", 1)
    down = from_behind(jnp.stack([left[0], kv[0, 0], kv[1, 0], right[0]]), "lat", -1)
    q = jnp.dot(grouped, w_qkv[:, :WIDTH], preferred_element_type=jnp.float32)
    q = q.astype(jnp.bfloat16).reshape(shape + (WIDTH,))
    meta, tables = bias_inputs(bias_table, index_table, pad_mask, lax.axis_index("lat"), lat_total)
    bias = pl.pallas_call(
        bias_kernel,
        out_shape=jax.ShapeDtypeStruct((2, 2, 3, 72, 8, 256), jnp.float32),
        in_specs=[pl.BlockSpec(memory_space=pltpu.VMEM)] * 2,
        out_specs=pl.BlockSpec(memory_space=pltpu.VMEM),
        compiler_params=pltpu.CompilerParams(vmem_limit_bytes=24 << 20),
        cost_estimate=pl.CostEstimate(
            flops=2 * 82 * 624 * 256 * 256, bytes_accessed=8 << 20, transcendentals=0
        ),
        name="bias",
    )(meta, tables)
    vectors = jnp.stack([proj_bias, norm_gain, norm_shift])
    whole = pl.BlockSpec(memory_space=pltpu.VMEM)

    def bias_block(i):
        quarter, lon = i // 2, i % 2
        return (1 - quarter % 2, (quarter + 1) // 2 % 2, 0, 1 - lon, 0, 0)

    out = pl.pallas_call(
        attend_kernel,
        grid=(8,),
        out_shape=jax.ShapeDtypeStruct((levels * lat_rows, lon_columns, features), jnp.bfloat16),
        in_specs=[pl.BlockSpec((1, 1, 3, GROUP, 8, 256), bias_block)] + [whole] * 10,
        out_specs=whole,
        scratch_shapes=[
            pltpu.VMEM((6, 2, WIN_TOK, 2 * WIDTH), jnp.bfloat16),
            pltpu.VMEM((rows, WIDTH), jnp.bfloat16),
        ],
        compiler_params=pltpu.CompilerParams(
            vmem_limit_bytes=40 << 20, dimension_semantics=("arbitrary",)
        ),
        name="attend",
    )(bias, q, kv, left, right, up, down, hidden, restore, w_proj, vectors)
    return out.reshape(state_tokens.shape)


def solution(mesh):
    in_specs = (
        P("member", "lat", "lon", None),
        P("lat", "lon"),
        P(),
        P(),
        P(),
        P(),
        P(),
        P(),
        P(),
        P("lat", None, None, None),
        P(),
    )
    out_specs = P("member", "lat", "lon", None)
    return jax.shard_map(
        on_device, mesh=mesh, in_specs=in_specs, out_specs=out_specs, check_vma=False
    )
```

time: 161 us -> 130 us (0.81)
  local copies, waits for them, and re-layouts: 101 us -> 40.3 us
  Pallas kernels: 0 us -> 35.1 us
  other arithmetic: 6.19 us -> 37.6 us
  waiting for transfers between devices: 30 us -> 0.01 us
  matrix products: 15.5 us -> 7.88 us
    gather x4 -> x0, local copies, waits for them, and re-layouts: 62.4 us -> none  [earth_bias(): picked = jnp.take(table_rows, index_table.reshape(-1), axis=0)]
    pallas_call x0 -> x2, Pallas kernels: none -> 35.1 us  [the longest x1 20.1 us: on_device(): pl.pallas_call(bias_kernel, out_shape=jax.ShapeDtypeStruct((2, 2, 3, 72,...]
    convert_element_type x3 -> x6, other arithmetic: 0.78 us -> 31.9 us  [the longest x4 30.2 us: allowed_pairs(): rows.append(((usable == 1) & same_row & same_level).astype(jnp.int32))]
    ppermute x4 -> x5, waiting for transfers between devices: 30 us -> 0.01 us  [from_behind(): lax.ppermute(shard, axis, [(i, (i + by) % size) for i in range(size)])]
    sub x1 -> x0, matrix products: 8.11 us -> none  [attend(): powers = jnp.exp(scores - largest)]
    reshape x5 -> x13, local copies, waits for them, and re-layouts: 1.84 us -> 9.07 us  [the longest x6 3.91 us: as_tiles(): main = rows[:, :128].reshape(72, 256)]
    unnamed x28 -> x89, local copies, waits for them, and re-layouts: 12.2 us -> 4.98 us
    convert_element_type x2 -> x0, local copies, waits for them, and re-layouts: 5.78 us -> none  [the longest x1 4.18 us: attend(): attended = jnp.einsum('abchtu,abcuhd->abcthd', weights, value_rows, prefe...]
  transfers between devices with their start and end apart: 4 -> 5, of which waited for: 3 -> 0; matrix products, arithmetic and copies ran while one was open for 41% -> 60% of each run, Pallas kernels for 0% -> 16%
where the time goes in v1:
time: 130 us; the launch traced here: 128 us
  local copies, waits for them, and re-layouts  40.3 us (31%)
  other arithmetic  37.6 us (29%)
  Pallas kernels  35.1 us (27%)
  matrix products  7.88 us (6%)
  starting transfers between devices  6.65 us (5%)
    convert_element_type x4, other arithmetic, allowed_pairs(): rows.append(((usable == 1) & same_row & same_level).astype(jnp.int32))  30.2 us
    pallas_call x1, Pallas kernels, on_device(): pl.pallas_call(bias_kernel, out_shape=jax.ShapeDtypeStruct((2, 2, 3, 72,...  20.1 us
    pallas_call x1, Pallas kernels, on_device(): pl.pallas_call(attend_kernel, grid=(8,), out_shape=jax.ShapeDtypeStruct((...  15 us
    another operation x7, local copies, waits for them, and re-layouts, bias_inputs(): meta = jnp.stack([as_tiles(r) for r in rows], axis=1)  7.01 us
    ppermute x5, starting transfers between devices, from_behind(): lax.ppermute(shard, axis, [(i, (i + by) % size) for i in range(size)])  6.65 us
    unnamed x89, local copies, waits for them, and re-layouts  4.98 us
    another operation x2, local copies, waits for them, and re-layouts, bias_inputs(): tables = jnp.stack([jnp.stack([third, second]), jnp.stack([first, second])])  3.93 us
    reshape x6, local copies, waits for them, and re-layouts, as_tiles(): main = rows[:, :128].reshape(72, 256)  3.91 us
  transfers between devices with their start and end apart: 5, of which 0 were waited for; matrix products, arithmetic and copies ran while one was open for 60% of the time, Pallas kernels for 16%

profile of v1, /device:TPU:0, one launch (start us, length us, event | category | flops | bytes accessed | tf_op | source)
XLA Modules:
  0.0 128.5 jit_solution(4783770494172053662)
XLA Ops:
  0.0 1.3 %fusion.87 = (bf16[1,2,12,3312]{3,1,2,0:T(2,128)(2,1)S(1)}, bf16[1,2,12,3312]{3,1,2,0:T(2,128)(2,1)S(1)}) fusion(bf16[2,2,12,3312]{3,1,2,0:T(2,128)(2,1)} %param.32), kind=kLoop, calls=%fused_computation.156 | loop fusion | bytes 635904 | tf_op jit(solution)/shard_map/slice | solution.py:291
  1.3 0.7 copy.43
  2.5 0.8 slice_reduce_fusion.1
  3.3 0.7 broadcast_compare_fusion
  5.4 1.2 fusion.2
  6.9 1.1 convolution_convert_fusion
  8.1 1.1 fusion.84
  9.2 2.5 %collective-permute-start.1 = (bf16[4,2,48,768]{3,2,1,0:T(8,128)(2,1)}, bf16[4,2,48,768]{3,2,1,0:T(8,128)(2,1)}, u32[]{:S(2)}, u32[]{:S(2)}) collective-permute-start(bf16[4,2,48,768]{3,2,1,0:T(8,128)(2,1)} %bitcast.49), channel_id=1, source_target_pairs={{0,2},{2,4},{4,6},{6,8},{8,10},{10,12},{12,14},{14,0},{1,3},{3,5},... | collective-permute-start | bytes 1769480 | tf_op jit(solution)/shard_map/ppermute | solution.py:28
  11.7 3.0 %collective-permute-start.2 = (bf16[4,2,48,768]{3,2,1,0:T(8,128)(2,1)}, bf16[4,2,48,768]{3,2,1,0:T(8,128)(2,1)}, u32[]{:S(2)}, u32[]{:S(2)}) collective-permute-start(bf16[4,2,48,768]{3,2,1,0:T(8,128)(2,1)} %bitcast.50), channel_id=1, source_target_pairs={{0,14},{2,0},{4,2},{6,4},{8,6},{10,8},{12,10},{14,12},{1,15},{3,1}... | collective-permute-start | bytes 1769480 | tf_op jit(solution)/shard_map/ppermute | solution.py:28
  14.7 0.7 fusion.88
  15.4 0.7 fusion.89
  16.2 15.3 %and_convert_fusion.1 = (s32[144,144]{1,0:T(8,128)S(1)}, pred[144,144]{1,0:T(8,128)(4,1)S(1)}) fusion(pred[144,144]{1,0:T(8,128)(4,1)S(1)} %copy-done.23, pred[144,144]{1,0:T(8,128)(4,1)S(1)} %copy-done.22, pred[144]{0:T(512)(128)(4,1)S(1)} %get-tuple-element.11, s32[]{:T(128)} %bitcast.25, s32[]{:T(128)} %bitcast.24, s32[]{:T(128)} %bitcast.23, ...), kind=kLoop, calls=%fused_computation.106 | loop fusion | flops 1264896 | bytes 146544 | tf_op jit(solution)/shard_map/convert_element_type | solution.py:259
  31.5 14.9 %and_convert_fusion = (s32[144,144]{1,0:T(8,128)S(1)}, pred[144,144]{1,0:T(8,128)(4,1)S(1)}) fusion(pred[144,144]{1,0:T(8,128)(4,1)S(1)} %copy-done.23, pred[144,144]{1,0:T(8,128)(4,1)S(1)} %copy-done.22, pred[]{:T(512)S(6)} %ne.55, s32[]{:T(128)} %bitcast.25, s32[]{:T(128)} %bitcast.24, s32[]{:T(128)} %bitcast.23, s32[]{:T(128)} %bitcast.22, s32[]{:T(128)} %bitcast.21, ...), kind=kLoop, calls=%fused_computation.105 | loop fusion | flops 1119744 | bytes 146545 | tf_op jit(solution)/shard_map/convert_element_type | solution.py:259
  46.6 1.4 %convolution_convert_fusion.2 = s32[144,144]{1,0:T(8,128)S(1)} fusion(bf16[144,144]{1,0:T(8,128)(2,1)} %constant.132.clone, bf16[144,144]{1,0:T(8,128)(2,1)} %constant.131.clone, s32[144,144]{1,0:T(8,128)S(1)} %copy-done.39), kind=kOutput, calls=%fused_computation.34 | convolution fusion | flops 12317184 | bytes 248832 | tf_op jit(solution)/shard_map/dot_general | solution.py:276
  48.0 1.5 %convolution_convert_fusion.3 = s32[144,144]{1,0:T(8,128)S(1)} fusion(bf16[144,144]{1,0:T(8,128)(2,1)} %constant.132.clone, bf16[144,144]{1,0:T(8,128)(2,1)} %constant.131.clone, s32[144,144]{1,0:T(8,128)} %param.33), kind=kOutput, calls=%fused_computation.35 | convolution fusion | flops 12234240 | bytes 248832 | tf_op jit(solution)/shard_map/dot_general | solution.py:276
  49.5 1.6 %fusion.59 = (bf16[4,3328]{1,0:T(4,128)(2,1)}, bf16[4,3328]{1,0:T(4,128)(2,1)}) fusion(bf16[2,12,3312]{2,1,0:T(8,128)(2,1)} %bitcast.87), kind=kLoop, calls=%fused_computation.125 | loop fusion | bytes 212224 | tf_op jit(solution)/shard_map/squeeze | solution.py:288
  51.1 1.6 %pad_slice_fusion.8 = bf16[2,8,3328]{2,1,0:T(8,128)(2,1)} fusion(bf16[2,12,3312]{2,1,0:T(8,128)(2,1)} %bitcast.87), kind=kLoop, calls=%fused_computation.61 | loop fusion | bytes 265472 | tf_op jit(solution)/shard_map/slice | solution.py:289
  53.3 0.7 pad_slice_fusion.5
  54.0 2.7 %convolution_convert_fusion.1 = bf16[768,384]{1,0:T(8,128)(2,1)} fusion(bf16[768,768]{1,0:T(8,128)(2,1)S(1)} %copy-done.42, bf16[768,1152]{1,0:T(8,128)(2,1)} %param.27), kind=kOutput, calls=%fused_computation.31 | convolution fusion | flops 453279744 | bytes 2359296 | tf_op jit(solution)/shard_map/dot_general | solution.py:330
  56.8 0.7 reshape.96
  58.1 0.7 reshape.102
  58.8 0.7 reshape.100
  59.5 0.7 reshape.99
  60.9 0.7 reshape.105
  62.2 0.7 reshape.93
  64.4 0.8 slice_bitcast_fusion.1
  65.3 1.2 fusion.1.restore_ref
  66.9 0.8 maximum_bitcast_fusion.1
  67.6 0.7 stack.87
  68.3 0.7 stack.89
  69.0 0.7 stack.88
  69.7 0.7 stack.90
  70.4 0.7 stack.86
  71.1 0.7 stack.85
  72.9 2.9 %stack.91.meta_ref = s32[82,6,256]{2,1,0:T(8,128)} concatenate(s32[82,1,256]{2,1,0:T(1,128)} %stack.85, s32[82,1,256]{2,1,0:T(1,128)} %stack.86, s32[82,1,256]{2,1,0:T(1,128)} %stack.87, s32[82,1,256]{2,1,0:T(1,128)} %stack.88, s32[82,1,256]{2,1,0:T(1,128)} %stack.89, s32[82,1,256]{2,1,0:T(1,128)} %stack.90), dimensions={1} | concatenate | bytes 1007616 | tf_op jit(solution)/shard_map/stack | solution.py:281
  75.8 0.7 pad_maximum_fusion.4.vectors_ref
  76.6 0.9 fusion.63
  77.5 0.9 pad_slice_fusion.2
  78.4 1.9 %pad_maximum_fusion.3 = (bf16[2,3,8,3328]{3,2,1,0:T(8,128)(2,1)}, bf16[2,3,8,3328]{3,2,1,0:T(8,128)(2,1)}) fusion(bf16[1,3,8,3328]{3,2,1,0:T(8,128)(2,1)} %get-tuple-element.60, bf16[1,3,8,3328]{3,2,1,0:T(8,128)(2,1)} %get-tuple-element.59, bf16[1,3,8,3328]{3,2,1,0:T(8,128)(2,1)S(1)} %maximum_bitcast_fusion.3), kind=kLoop, calls=%fused_computation.43 | loop fusion | flops 319488 | bytes 1118208 | tf_op jit(solution)/shard_map/stack | solution.py:292
  80.3 2.0 %stack.104 = bf16[1,48,13,256]{3,2,1,0:T(8,128)(2,1)} reshape(bf16[2,3,8,3328]{3,2,1,0:T(8,128)(2,1)} %get-tuple-element.32) | data formatting | bytes 638976 | tf_op jit(solution)/shard_map/stack | solution.py:292
  82.2 2.0 %stack.99 = bf16[1,48,13,256]{3,2,1,0:T(8,128)(2,1)} reshape(bf16[2,3,8,3328]{3,2,1,0:T(8,128)(2,1)} %get-tuple-element.31) | data formatting | bytes 638976 | tf_op jit(solution)/shard_map/stack | solution.py:292
  84.2 1.2 maximum_bitcast_fusion
  85.7 1.0 fusion.85
  86.7 1.0 fusion.86
  88.9 20.1 %bias.1.bias_ref = f32[2,2,3,72,8,256]{5,4,3,2,1,0:T(8,128)S(1)} custom-call(s32[82,6,256]{2,1,0:T(8,128)S(1)} %copy-done.1, bf16[2,624,256]{2,1,0:T(8,128)(2,1)S(1)} %bitcast.93), custom_call_target="tpu_custom_call" | custom-call | flops 6706692096 | bytes 8388608 | tf_op jit(solution)/shard_map/bias/pallas_call | solution.py:333
  109.0 2.8 %copy-done = f32[2,2,3,72,8,256]{5,4,3,2,1,0:T(8,128)} copy-done((f32[2,2,3,72,8,256]{5,4,3,2,1,0:T(8,128)}, f32[2,2,3,72,8,256]{5,4,3,2,1,0:T(8,128)S(1)}, u32[]{:S(2)}) %copy-start) | copy-done | bytes 7077912
  111.8 15.0 %attend.1 = bf16[48,12,768]{2,1,0:T(8,128)(2,1)S(1)} custom-call(f32[2,2,3,72,8,256]{5,4,3,2,1,0:T(8,128)} %copy-done, bf16[2,4,2,48,384]{4,3,2,1,0:T(8,128)(2,1)S(1)} %bitcast.94, bf16[2,4,2,48,768]{4,3,2,1,0:T(8,128)(2,1)S(1)} %bitcast.89, bf16[4,2,48,768]{3,2,1,0:T(8,128)(2,1)} %collective-permute-done.1.left_ref, ...), custom_call_target="tpu_custom_call" | custom-call | tf_op jit(solution)/shard_map/attend/pallas_call | solution.py:351
  126.9 1.6 %copy.36 = bf16[4,12,12,768]{3,0,2,1:T(4,128)(2,1)} copy(bf16[4,12,12,768]{3,2,1,0:T(8,128)(2,1)S(1)} %bitcast.92) | data formatting | bytes 1769472 | tf_op jit(solution)/shard_map/reshape | solution.py:366
  (153 shorter events, 9.2 us)
Async XLA Ops:
  0.0 4.1 %copy-start.4 = (bf16[4,12,12,768]{3,0,2,1:T(4,128)(2,1)S(1)}, bf16[4,12,12,768]{3,0,2,1:T(4,128)(2,1)}, u32[]{:S(2)}) copy-start(bf16[4,12,12,768]{3,0,2,1:T(4,128)(2,1)} %param.23) | copy-start | bytes 2654212
  2.0 74.5 %collective-permute-start = (bf16[2,12,3312]{2,1,0:T(8,128)(2,1)}, bf16[2,12,3312]{2,1,0:T(8,128)(2,1)}, u32[]{:S(2)}, u32[]{:S(2)}) collective-permute-start(bf16[2,12,3312]{2,1,0:T(8,128)(2,1)} %bitcast.87), channel_id=1, source_target_pairs={{0,1},{1,0},{2,3},{3,2},{4,5},{5,4},{6,7},{7,6},{8,9},{9,8},{10,11... | collective-permute-start | bytes 476936 | tf_op jit(solution)/shard_map/ppermute | solution.py:28
  8.0 6.7 %copy-start.13 = (s32[24]{0:T(128)S(1)}, s32[24]{0:T(128)}, u32[]{:S(2)}) copy-start(s32[24]{0:T(128)} %param.25) | copy-start | bytes 292
  8.0 8.1 %copy-start.37 = (pred[144]{0:T(512)(128)(4,1)S(1)}, pred[144]{0:T(512)(128)(4,1)}, u32[]{:S(2)}) copy-start(pred[144]{0:T(512)(128)(4,1)} %constant.133.clone) | copy-start | bytes 436
  8.0 8.1 %copy-start.22 = (pred[144,144]{1,0:T(8,128)(4,1)S(1)}, pred[144,144]{1,0:T(8,128)(4,1)}, u32[]{:S(2)}) copy-start(pred[144,144]{1,0:T(8,128)(4,1)} %constant.135.clone) | copy-start | bytes 62212
  8.0 8.1 %copy-start.23 = (pred[144,144]{1,0:T(8,128)(4,1)S(1)}, pred[144,144]{1,0:T(8,128)(4,1)}, u32[]{:S(2)}) copy-start(pred[144,144]{1,0:T(8,128)(4,1)} %constant.137.clone) | copy-start | bytes 62212
  8.1 8.1 %copy-start.33 = (s32[144]{0:T(256)S(1)}, s32[144]{0:T(256)}, u32[]{:S(2)}) copy-start(s32[144]{0:T(256)} %constant.134.clone) | copy-start | bytes 1732
  9.2 37.4 %copy-start.39 = (s32[144,144]{1,0:T(8,128)S(1)}, s32[144,144]{1,0:T(8,128)}, u32[]{:S(2)}) copy-start(s32[144,144]{1,0:T(8,128)} %param.33) | copy-start | bytes 248836
  9.2 76.5 %collective-permute-start.1 = (bf16[4,2,48,768]{3,2,1,0:T(8,128)(2,1)}, bf16[4,2,48,768]{3,2,1,0:T(8,128)(2,1)}, u32[]{:S(2)}, u32[]{:S(2)}) collective-permute-start(bf16[4,2,48,768]{3,2,1,0:T(8,128)(2,1)} %bitcast.49), channel_id=1, source_target_pairs={{0,2},{2,4},{4,6},{6,8},{8,10},{10,12},{12,14},{14,0},{1,3},{3,5},... | collective-permute-start | bytes 1769480 | tf_op jit(solution)/shard_map/ppermute | solution.py:28
  11.7 75.1 %collective-permute-start.2 = (bf16[4,2,48,768]{3,2,1,0:T(8,128)(2,1)}, bf16[4,2,48,768]{3,2,1,0:T(8,128)(2,1)}, u32[]{:S(2)}, u32[]{:S(2)}) collective-permute-start(bf16[4,2,48,768]{3,2,1,0:T(8,128)(2,1)} %bitcast.50), channel_id=1, source_target_pairs={{0,14},{2,0},{4,2},{6,4},{8,6},{10,8},{12,10},{14,12},{1,15},{3,1}... | collective-permute-start | bytes 1769480 | tf_op jit(solution)/shard_map/ppermute | solution.py:28
  31.5 16.5 %copy-start.9 = (s32[144,144]{1,0:T(8,128)}, s32[144,144]{1,0:T(8,128)S(1)}, u32[]{:S(2)}) copy-start(s32[144,144]{1,0:T(8,128)S(1)} %convert_element_type.63) | copy-start | bytes 248836
  46.5 3.0 %copy-start.10 = (s32[144,144]{1,0:T(8,128)}, s32[144,144]{1,0:T(8,128)S(1)}, u32[]{:S(2)}) copy-start(s32[144,144]{1,0:T(8,128)S(1)} %convert_element_type.65) | copy-start | bytes 248836
  48.0 5.3 %copy-start.15 = (s32[144,144]{1,0:T(8,128)}, s32[144,144]{1,0:T(8,128)S(1)}, u32[]{:S(2)}) copy-start(s32[144,144]{1,0:T(8,128)S(1)} %convolution_convert_fusion.2) | copy-start | bytes 248836
  49.5 7.2 %copy-start.14 = (s32[144,144]{1,0:T(8,128)}, s32[144,144]{1,0:T(8,128)S(1)}, u32[]{:S(2)}) copy-start(s32[144,144]{1,0:T(8,128)S(1)} %convolution_convert_fusion.3) | copy-start | bytes 248836
  49.5 4.5 %copy-start.42 = (bf16[768,768]{1,0:T(8,128)(2,1)S(1)}, bf16[768,768]{1,0:T(8,128)(2,1)}, u32[]{:S(2)}) copy-start(bf16[768,768]{1,0:T(8,128)(2,1)} %copy-done.41) | copy-start | bytes 3538948
  54.0 2.7 %slice-start = ((s32[144,144]{1,0:T(8,128)}), s32[144,16]{1,0:T(8,128)S(1)}, s32[]{:S(2)}) async-start(s32[144,144]{1,0:T(8,128)} %copy-done.9), calls=%async_computation | async-start | bytes 147456 | tf_op jit(solution)/shard_map/slice | solution.py:265
  54.0 3.5 %slice-start.1 = ((s32[144,144]{1,0:T(8,128)}), s32[144,128]{1,0:T(8,128)S(1)}, s32[]{:S(2)}) async-start(s32[144,144]{1,0:T(8,128)} %copy-done.9), calls=%async_computation.1 | async-start | bytes 147456 | tf_op jit(solution)/shard_map/slice | solution.py:264
  54.0 4.1 %slice-start.2 = ((s32[144,144]{1,0:T(8,128)}), s32[144,16]{1,0:T(8,128)S(1)}, s32[]{:S(2)}) async-start(s32[144,144]{1,0:T(8,128)} %copy-done.10), calls=%async_computation.2 | async-start | bytes 147456 | tf_op jit(solution)/shard_map/slice | solution.py:265
  54.0 4.8 %slice-start.3 = ((s32[144,144]{1,0:T(8,128)}), s32[144,128]{1,0:T(8,128)S(1)}, s32[]{:S(2)}) async-start(s32[144,144]{1,0:T(8,128)} %copy-done.10), calls=%async_computation.3 | async-start | bytes 147456 | tf_op jit(solution)/shard_map/slice | solution.py:264
  56.7 5.5 %slice-start.6 = ((s32[144,144]{1,0:T(8,128)}), s32[144,16]{1,0:T(8,128)S(1)}, s32[]{:S(2)}) async-start(s32[144,144]{1,0:T(8,128)} %copy-done.15), calls=%async_computation.6 | async-start | bytes 147456 | tf_op jit(solution)/shard_map/slice | solution.py:265
  56.7 6.2 %slice-start.7 = ((s32[144,144]{1,0:T(8,128)}), s32[144,128]{1,0:T(8,128)S(1)}, s32[]{:S(2)}) async-start(s32[144,144]{1,0:T(8,128)} %copy-done.15), calls=%async_computation.7 | async-start | bytes 147456 | tf_op jit(solution)/shard_map/slice | solution.py:264
  56.7 6.8 %slice-start.4 = ((s32[144,144]{1,0:T(8,128)}), s32[144,16]{1,0:T(8,128)S(1)}, s32[]{:S(2)}) async-start(s32[144,144]{1,0:T(8,128)} %copy-done.14), calls=%async_computation.4 | async-start | bytes 147456 | tf_op jit(solution)/shard_map/slice | solution.py:265
  56.7 6.9 %slice-start.5 = ((s32[144,144]{1,0:T(8,128)}), s32[144,128]{1,0:T(8,128)S(1)}, s32[]{:S(2)}) async-start(s32[144,144]{1,0:T(8,128)} %copy-done.14), calls=%async_computation.5 | async-start | bytes 147456 | tf_op jit(solution)/shard_map/slice | solution.py:264
  64.3 2.2 %copy-start.16 = (s32[72,256]{1,0:T(8,128)S(1)}, s32[72,256]{1,0:T(8,128)}, u32[]{:S(2)}) copy-start(s32[72,256]{1,0:T(8,128)} %reshape.94) | copy-start | bytes 221188
  64.3 2.2 %copy-start.28 = (s32[10,256]{1,0:T(8,128)S(1)}, s32[10,256]{1,0:T(8,128)}, u32[]{:S(2)}) copy-start(s32[10,256]{1,0:T(8,128)} %reshape.96) | copy-start | bytes 30724
  64.3 2.2 %copy-start.18 = (s32[72,256]{1,0:T(8,128)S(1)}, s32[72,256]{1,0:T(8,128)}, u32[]{:S(2)}) copy-start(s32[72,256]{1,0:T(8,128)} %reshape.100) | copy-start | bytes 221188
  64.3 2.2 %copy-start.29 = (s32[10,256]{1,0:T(8,128)S(1)}, s32[10,256]{1,0:T(8,128)}, u32[]{:S(2)}) copy-start(s32[10,256]{1,0:T(8,128)} %reshape.102) | copy-start | bytes 30724
  64.3 2.2 %copy-start.19 = (s32[72,256]{1,0:T(8,128)S(1)}, s32[72,256]{1,0:T(8,128)}, u32[]{:S(2)}) copy-start(s32[72,256]{1,0:T(8,128)} %reshape.97) | copy-start | bytes 221188
  64.4 2.2 %copy-start.30 = (s32[10,256]{1,0:T(8,128)S(1)}, s32[10,256]{1,0:T(8,128)}, u32[]{:S(2)}) copy-start(s32[10,256]{1,0:T(8,128)} %reshape.99) | copy-start | bytes 30724
  64.4 2.2 %copy-start.20 = (s32[72,256]{1,0:T(8,128)S(1)}, s32[72,256]{1,0:T(8,128)}, u32[]{:S(2)}) copy-start(s32[72,256]{1,0:T(8,128)} %reshape.103) | copy-start | bytes 221188
  64.4 2.2 %copy-start.31 = (s32[10,256]{1,0:T(8,128)S(1)}, s32[10,256]{1,0:T(8,128)}, u32[]{:S(2)}) copy-start(s32[10,256]{1,0:T(8,128)} %reshape.105) | copy-start | bytes 30724
  65.2 1.5 %copy-start.26 = (bf16[4,3328]{1,0:T(4,128)(2,1)S(1)}, bf16[4,3328]{1,0:T(4,128)(2,1)}, u32[]{:S(2)}) copy-start(bf16[4,3328]{1,0:T(4,128)(2,1)} %get-tuple-element.29) | copy-start | bytes 79876
  65.2 1.5 %copy-start.27 = (bf16[4,3328]{1,0:T(4,128)(2,1)S(1)}, bf16[4,3328]{1,0:T(4,128)(2,1)}, u32[]{:S(2)}) copy-start(bf16[4,3328]{1,0:T(4,128)(2,1)} %get-tuple-element.30) | copy-start | bytes 79876
  65.3 1.6 %copy-start.11 = (bf16[2,8,3328]{2,1,0:T(8,128)(2,1)S(1)}, bf16[2,8,3328]{2,1,0:T(8,128)(2,1)}, u32[]{:S(2)}) copy-start(bf16[2,8,3328]{2,1,0:T(8,128)(2,1)} %pad_slice_fusion.8) | copy-start | bytes 319492
  65.3 1.6 %copy-start.12 = (bf16[2,8,3328]{2,1,0:T(8,128)(2,1)S(1)}, bf16[2,8,3328]{2,1,0:T(8,128)(2,1)}, u32[]{:S(2)}) copy-start(bf16[2,8,3328]{2,1,0:T(8,128)(2,1)} %pad_slice_fusion.5) | copy-start | bytes 319492
  65.3 2.4 %copy-start.17 = (s32[72,256]{1,0:T(8,128)S(1)}, s32[72,256]{1,0:T(8,128)}, u32[]{:S(2)}) copy-start(s32[72,256]{1,0:T(8,128)} %reshape.88) | copy-start | bytes 221188
  66.6 5.1 %copy-start.34 = (f32[768]{0:T(1024)S(1)}, f32[768]{0:T(1024)}, u32[]{:S(2)}) copy-start(f32[768]{0:T(1024)} %param.29) | copy-start | bytes 9220
  66.7 5.1 %copy-start.35 = (f32[768]{0:T(1024)S(1)}, f32[768]{0:T(1024)}, u32[]{:S(2)}) copy-start(f32[768]{0:T(1024)} %param.30) | copy-start | bytes 9220
  66.7 5.7 %copy-start.36 = (f32[768]{0:T(1024)S(1)}, f32[768]{0:T(1024)}, u32[]{:S(2)}) copy-start(f32[768]{0:T(1024)} %param.31) | copy-start | bytes 9220
  85.4 2.3 %copy-start.7 = (bf16[1,2,48,768]{3,2,1,0:T(8,128)(2,1)S(1)}, bf16[1,2,48,768]{3,2,1,0:T(8,128)(2,1)}, u32[]{:S(2)}) copy-start(bf16[1,2,48,768]{3,2,1,0:T(8,128)(2,1)} %get-tuple-element.13) | copy-start | bytes 442372
  85.4 2.3 %copy-start.8 = (bf16[1,2,48,768]{3,2,1,0:T(8,128)(2,1)S(1)}, bf16[1,2,48,768]{3,2,1,0:T(8,128)(2,1)}, u32[]{:S(2)}) copy-start(bf16[1,2,48,768]{3,2,1,0:T(8,128)(2,1)} %get-tuple-element.14) | copy-start | bytes 442372
  85.7 2.5 %copy-start.5 = (bf16[1,2,48,768]{3,2,1,0:T(8,128)(2,1)S(1)}, bf16[1,2,48,768]{3,2,1,0:T(8,128)(2,1)}, u32[]{:S(2)}) copy-start(bf16[1,2,48,768]{3,2,1,0:T(8,128)(2,1)} %get-tuple-element.15) | copy-start | bytes 442372
  85.7 2.5 %copy-start.6 = (bf16[1,2,48,768]{3,2,1,0:T(8,128)(2,1)S(1)}, bf16[1,2,48,768]{3,2,1,0:T(8,128)(2,1)}, u32[]{:S(2)}) copy-start(bf16[1,2,48,768]{3,2,1,0:T(8,128)(2,1)} %get-tuple-element.16) | copy-start | bytes 442372
  87.9 23.9 %collective-permute-start.4 = (bf16[4,2,48,768]{3,2,1,0:T(8,128)(2,1)S(1)}, bf16[4,2,48,768]{3,2,1,0:T(8,128)(2,1)S(1)}, u32[]{:S(2)}, u32[]{:S(2)}) collective-permute-start(bf16[4,2,48,768]{3,2,1,0:T(8,128)(2,1)S(1)} %pad_maximum_fusion.1), channel_id=1, source_target_pairs={{0,1},{1,0},{2,3},{3,2},{4,5},{5,4},{6,7},{7,6},{8,9},{9,8},{10,11... | collective-permute-start | bytes 1769480 | tf_op jit(solution)/shard_map/ppermute | solution.py:28
  88.2 23.6 %collective-permute-start.3 = (bf16[4,2,48,768]{3,2,1,0:T(8,128)(2,1)S(1)}, bf16[4,2,48,768]{3,2,1,0:T(8,128)(2,1)S(1)}, u32[]{:S(2)}, u32[]{:S(2)}) collective-permute-start(bf16[4,2,48,768]{3,2,1,0:T(8,128)(2,1)S(1)} %pad_maximum_fusion), channel_id=1, source_target_pairs={{0,1},{1,0},{2,3},{3,2},{4,5},{5,4},{6,7},{7,6},{8,9},{9,8},{10,11... | collective-permute-start | bytes 1769480 | tf_op jit(solution)/shard_map/ppermute | solution.py:28
  88.9 23.0 %copy-start.2 = (bf16[384,768]{1,0:T(8,128)(2,1)S(1)}, bf16[384,768]{1,0:T(8,128)(2,1)}, u32[]{:S(2)}) copy-start(bf16[384,768]{1,0:T(8,128)(2,1)} %w_ref.1) | copy-start | bytes 1769476
  88.9 23.0 %copy-start.3 = (bf16[768,384]{1,0:T(8,128)(2,1)S(1)}, bf16[768,384]{1,0:T(8,128)(2,1)}, u32[]{:S(2)}) copy-start(bf16[768,384]{1,0:T(8,128)(2,1)} %convolution_convert_fusion.1) | copy-start | bytes 1769476
  109.0 2.8 %copy-start = (f32[2,2,3,72,8,256]{5,4,3,2,1,0:T(8,128)}, f32[2,2,3,72,8,256]{5,4,3,2,1,0:T(8,128)S(1)}, u32[]{:S(2)}) copy-start(f32[2,2,3,72,8,256]{5,4,3,2,1,0:T(8,128)S(1)} %bias.1.bias_ref) | copy-start | bytes 21233668
  (8 other events, 10.2 us)

commit v2 on v1

--- a/solution.py
+++ b/solution.py
@@ -69,55 +69,138 @@
     return placed, plain
 
 
-def bias_kernel(meta_ref, table_ref, out_ref):
+def bias_kernel(
+    index_ref,
+    before_ref,
+    own_ref,
+    pad_ref,
+    lat_ref,
+    to_q_ref,
+    to_k_ref,
+    to_q_rest_ref,
+    to_k_rest_ref,
+    geometry_ref,
+    out_ref,
+    low_ref,
+    high_ref,
+    table_ref,
+):
+    positions = own_ref.shape[-1]
     highs = table_ref.shape[1] // 48
     half_row = lax.broadcasted_iota(jnp.int32, (8, LOW), 0) < 4
     low_iota = lax.broadcasted_iota(jnp.int32, (LOW, LOW), 0)
 
-    def look_up(a, tile):
-        meta = meta_ref[tile]
-        hot = jnp.where(low_iota == meta[0:1], 1.0, 0.0).astype(jnp.bfloat16)
-        found = jnp.dot(table_ref[a], hot, preferred_element_type=jnp.float32)
-        high = jnp.broadcast_to(meta[1:2], (48, LOW))
+    def dot(x, y):
+        return jnp.dot(x, y, preferred_element_type=jnp.float32)
+
+    index = index_ref[...]
+    rest_lane = lax.broadcasted_iota(jnp.int32, (160, LOW), 1) // 16
+    rest_row = lax.broadcasted_iota(jnp.int32, (160, LOW), 0) % 16
+    gather = jnp.where(
+        lax.broadcasted_iota(jnp.int32, (16, 160), 1) // 16
+        == lax.broadcasted_iota(jnp.int32, (16, 160), 0),
+        1.0,
+        0.0,
+    ).astype(jnp.bfloat16)
+    for values, ref in ((index % LOW, low_ref), (index // LOW, high_ref)):
+        values = values.astype(jnp.float32).astype(jnp.bfloat16)
+        main = dot(dot(to_q_ref[...], values).astype(jnp.bfloat16), to_k_ref[...])
+        ref[0:WIN_TOK, :] = main.astype(jnp.int32)
+        rest = dot(dot(to_q_rest_ref[...], values).astype(jnp.bfloat16), to_k_rest_ref[...])
+        rest = jnp.where(rest_lane == rest_row, rest, 0.0).astype(jnp.bfloat16)
+        rest = dot(gather, rest).astype(jnp.int32)
+        ref[WIN_TOK : WIN_TOK + 16, :] = rest[:, 0:128]
+        ref[WIN_TOK + 16 : WIN_TOK + 32, :] = rest[:, 128:256]
+
+    for k in range(highs):
+        end = min(positions, (k + 1) * LOW)
+        sides = []
+        for window in range(3):
+            parts = []
+            for zw in range(WIN_Z):
+                ref = before_ref if window == 0 else own_ref.at[window - 1]
+                part = ref[zw, :, k * LOW : end].astype(jnp.float32)
+                if end < (k + 1) * LOW:
+                    fill = jnp.zeros((part.shape[0], (k + 1) * LOW - end), jnp.float32)
+                    part = jnp.concatenate([part, fill], axis=1)
+                parts.append(part)
+            sides.append([parts[0][:8], parts[1][:8], parts[0][8:], parts[1][8:]])
+        for a, edge in ((0, 2), (1, 0)):
+            block = jnp.concatenate(sides[edge] + sides[1], axis=0)
+            table_ref[a, k * 48 : (k + 1) * 48, :] = block.astype(jnp.bfloat16)
+
+    lat_total = pad_ref.shape[0]
+    windows = lat_total // WIN_LAT
+    base = 2 * lat_ref[0]
+
+    def look_up(a, tile, low, high):
+        hot = jnp.where(low_iota == low, 1.0, 0.0).astype(jnp.bfloat16)
+        found = dot(table_ref[a], hot)
+        high = jnp.broadcast_to(high, (48, LOW))
         total = found[0:48]
         for k in range(1, highs):
             total = jnp.where(high == k, found[k * 48 : (k + 1) * 48], total)
+        geometry = geometry_ref[tile]
+        key_row, same_half, same_level = geometry[0:1], geometry[1:2], geometry[2:3]
         pieces = []
         for s in range(2):
-            first = jnp.broadcast_to(meta[2 + 2 * s : 3 + 2 * s], (8, LOW))
-            second = jnp.broadcast_to(meta[3 + 2 * s : 4 + 2 * s], (8, LOW))
+            window = base
+            if s == 0:
+                window = lax.rem(base - 1 + windows if a == 1 else base + 1, windows)
+            usable = jnp.zeros((1, LOW), jnp.int32)
+            for n in range(WIN_LAT):
+                source = lax.rem(window * WIN_LAT + n + HALF_LAT, lat_total)
+                usable = jnp.where(key_row == n, pad_ref[source], usable)
+            inner = (window != windows - 1).astype(jnp.int32)
+            usable = jnp.where(usable == 1, jnp.maximum(same_half, inner), 0)
+            first = jnp.broadcast_to(usable, (8, LOW))
+            second = jnp.broadcast_to(usable * same_level, (8, LOW))
             for kind, allowed in enumerate((first, second, jnp.where(half_row, first, second))):
                 part = total[(s * 3 + kind) * 8 : (s * 3 + kind) * 8 + 8]
                 pieces.append(jnp.where(allowed == 1, part, SHUT))
         return pieces
 
+    def both(x, y):
+        return jnp.concatenate([x, y], axis=0).astype(jnp.bfloat16)
+
     for a in range(2):
 
         def pair(p, carry, a=a):
-            pieces = look_up(a, a * 36 + p)
+            tile = a * 36 + p
+
+            def two(ref):
+                return jnp.concatenate(
+                    [ref[pl.ds(2 * tile, 1), :], ref[pl.ds(2 * tile + 1, 1), :]], axis=1
+                )
+
+            pieces = look_up(a, tile, two(low_ref), two(high_ref))
             for s in range(2):
                 for kind in range(3):
                     part = pieces[s * 3 + kind]
-                    out_ref[a, s, kind, 2 * p, :, 0:128] = part[:, 0:128]
-                    out_ref[a, s, kind, 2 * p + 1, :, 0:128] = part[:, 128:256]
+                    out_ref[a, s, kind, p, :, 0:128] = both(part[:, 0:128], part[:, 128:256])
             return carry
 
         lax.fori_loop(0, 36, pair, 0)
         for tile in range(5):
-            pieces = look_up(a, 72 + a * 5 + tile)
-            for j in range(16):
+            row = WIN_TOK + a * 5 + tile
+
+            def wide(ref, row=row):
+                return jnp.concatenate([ref[row : row + 1, :], ref[row + 16 : row + 17, :]], axis=1)
+
+            pieces = look_up(a, 72 + a * 5 + tile, wide(low_ref), wide(high_ref))
+            for j in range(0, 16, 2):
                 q = tile * 16 + j
                 if q < 72:
                     for s in range(2):
                         for kind in range(3):
-                            out_ref[a, s, kind, q, :, 128:144] = pieces[s * 3 + kind][
-                                :, 16 * j : 16 * j + 16
-                            ]
+                            part = pieces[s * 3 + kind]
+                            out_ref[a, s, kind, q // 2, :, 128:144] = both(
+                                part[:, 16 * j : 16 * j + 16], part[:, 16 * j + 16 : 16 * j + 32]
+                            )
 
 
 def attend_kernel(
     bias_ref,
-    q_ref,
     own_ref,
     left_ref,
     right_ref,
@@ -126,7 +209,9 @@
     hidden_ref,
     restore_ref,
     w_ref,
-    vectors_ref,
+    offset_ref,
+    gain_ref,
+    shift_ref,
     out_ref,
     keys_ref,
     attended_ref,
@@ -144,7 +229,7 @@
                 return left_ref.at[quarter, zw]
             if c == 3:
                 return right_ref.at[quarter, zw]
-            return own_ref.at[c - 1, quarter, zw]
+            return own_ref.at[c - 1, quarter, zw, :, WIDTH : 3 * WIDTH]
 
         for lat in range(3):
             for lon in range(2):
@@ -175,7 +260,7 @@
     ).astype(jnp.bfloat16)
     queries = []
     for zw in range(2):
-        q = q_ref[lon, quarter, zw].astype(jnp.float32)
+        q = own_ref[lon, quarter, zw, :, 0:WIDTH].astype(jnp.float32)
         tail = (q[32:36] + q[36:40]) + (q[40:44] + q[44:48])
         queries.append(jnp.concatenate([q[0:32], tail], axis=0))
     results = []
@@ -197,6 +282,7 @@
             spread, key, (((1,), (1,)), ((), ())), preferred_element_type=jnp.float32
         )
         bias = bias_ref[0, 0, kind].reshape(8 * GROUP, 256)[:, 0:WIN_TOK]
+        bias = bias.astype(jnp.float32)
         scores = scores * (HEAD_DIM**-0.5) + bias
         powers = jnp.exp(scores - jnp.max(scores, axis=-1, keepdims=True))
         weights = (powers / jnp.sum(powers, axis=-1, keepdims=True)).astype(jnp.bfloat16)
@@ -224,13 +310,13 @@
             ).astype(jnp.bfloat16)
             projected = (
                 jnp.dot(natural, w_ref[...], preferred_element_type=jnp.float32)
-                + vectors_ref[0:1, :]
+                + offset_ref[...]
             )
             centered = projected - jnp.mean(projected, axis=-1, keepdims=True)
             spread = jnp.mean(centered * centered, axis=-1, keepdims=True)
             normed = (
-                centered * lax.rsqrt(spread + norm_epsilon) * vectors_ref[1:2, :]
-                + vectors_ref[2:3, :]
+                centered * lax.rsqrt(spread + norm_epsilon) * gain_ref[...]
+                + shift_ref[...]
             )
             result = (hidden_ref[n : n + chunk, :].astype(jnp.float32) + normed).astype(
                 jnp.bfloat16
@@ -239,59 +325,30 @@
             out_ref[n // 16 : (n + chunk) // 16] = result[:, : out_ref.shape[1], :]
 
 
-def allowed_pairs(lat_index, lat_total, pad_mask):
+def as_tiles(rows):
+    main = rows[:, :128].reshape(72, 256)
+    rest = np.pad(rows[:, 128:].reshape(2, 72, 16), ((0, 0), (0, 8), (0, 0))).reshape(10, 256)
+    return np.concatenate([main, rest], axis=0)
+
+
+def bias_constants():
     queries, keys = window_orders()
-    windows = lat_total // WIN_LAT
+    eye = np.eye(WIN_TOK, dtype=np.float32)
+    to_q = eye[queries]
+    to_q_rest = np.pad(to_q.reshape(2, 72, WIN_TOK), ((0, 0), (0, 8), (0, 0)))
+    to_q_rest = to_q_rest.reshape(160, WIN_TOK)
+    to_k = eye[keys[:128]].T
+    to_k_rest = eye[np.tile(keys[128:], 16)].T
     q_level, q_half = queries // 72, queries // 12 % 6 // 3
     k_level, k_row = keys // 72, keys // 12 % 6
-    base = 2 * lat_index
-    edge = jnp.where(jnp.asarray(q_half == 1), base - 1 + windows, base + 1) % windows
-    rows = []
-    for window in (edge, jnp.zeros_like(edge) + base):
-        source = (window[:, None] * WIN_LAT + jnp.asarray(k_row)[None, :] + HALF_LAT) % lat_total
-        usable = jnp.zeros(source.shape, jnp.int32)
-        for n in range(pad_mask.shape[0]):
-            usable = jnp.where(source == n, pad_mask[n], usable)
-        same_half = jnp.asarray(q_half[:, None] == (k_row // 3)[None, :])
-        same_row = (window[:, None] != windows - 1) | same_half
-        for zw in range(2):
-            same_level = jnp.asarray((zw == 0) | (q_level[:, None] == k_level[None, :]))
-            rows.append(((usable == 1) & same_row & same_level).astype(jnp.int32))
-    return rows
-
-
-def as_tiles(rows):
-    main = rows[:, :128].reshape(72, 256)
-    rest = jnp.pad(rows[:, 128:].reshape(2, 72, 16), ((0, 0), (0, 8), (0, 0))).reshape(10, 256)
-    return jnp.concatenate([main, rest], axis=0)
-
-
-def bias_inputs(bias_table, index_table, pad_mask, lat_index, lat_total):
-    queries, keys = window_orders()
-    to_q = jnp.asarray(np.eye(WIN_TOK)[queries], jnp.bfloat16)
-    to_k = jnp.asarray(np.eye(WIN_TOK)[keys].T, jnp.bfloat16)
-
-    def reorder(values):
-        picked = jnp.dot(to_q, values.astype(jnp.bfloat16), preferred_element_type=jnp.float32)
-        picked = jnp.dot(picked.astype(jnp.bfloat16), to_k, preferred_element_type=jnp.float32)
-        return picked.astype(jnp.int32)
-
-    rows = [reorder(index_table % LOW), reorder(index_table // LOW)]
-    rows += allowed_pairs(lat_index, lat_total, pad_mask)
-    meta = jnp.stack([as_tiles(r) for r in rows], axis=1)
-    before = from_behind(bias_table[-1], "lat", 1)
-    positions = bias_table.shape[-1]
-    highs = -(-positions // LOW)
-
-    def kinds(table):
-        table = jnp.pad(table, ((0, 0), (0, 0), (0, highs * LOW - positions)))
-        last = jnp.concatenate([table[0, 8:], table[1, 8:]], axis=0)
-        return jnp.stack([table[0, :8], table[1, :8], last])
-
-    first, second, third = kinds(before), kinds(bias_table[0]), kinds(bias_table[1])
-    tables = jnp.stack([jnp.stack([third, second]), jnp.stack([first, second])])
-    tables = tables.reshape(2, 48, highs, LOW).transpose(0, 2, 1, 3).reshape(2, highs * 48, LOW)
-    return meta, tables
+    planes = [
+        np.broadcast_to(k_row[None, :], (WIN_TOK, WIN_TOK)),
+        q_half[:, None] == (k_row // 3)[None, :],
+        q_level[:, None] == k_level[None, :],
+    ]
+    geometry = np.stack([as_tiles(p.astype(np.int32)) for p in planes], axis=1)
+    matrices = [jnp.asarray(m, jnp.bfloat16) for m in (to_q, to_k, to_q_rest, to_k_rest)]
+    return matrices + [jnp.asarray(geometry)]
 
 
 def on_device(
@@ -321,27 +378,35 @@
     restore = (natural[:, None] == jnp.asarray(plain)[None, :]).astype(jnp.bfloat16)
     grouped = jnp.dot(to_groups, hidden, preferred_element_type=jnp.float32).astype(jnp.bfloat16)
     shape = (2, 4, 2, SLOT)
-    kv = jnp.dot(grouped, w_qkv[:, WIDTH:], preferred_element_type=jnp.float32)
-    kv = kv.astype(jnp.bfloat16).reshape(shape + (2 * WIDTH,))
+    qkv = jnp.dot(grouped, w_qkv, preferred_element_type=jnp.float32)
+    qkv = qkv.astype(jnp.bfloat16).reshape(2, 4, 2, SLOT, 3 * WIDTH)
+    kv = qkv[..., WIDTH:]
     right = from_behind(kv[0], "lon", -1)
     left = from_behind(kv[1], "lon", 1)
     up = from_behind(jnp.stack([left[3], kv[0, 3], kv[1, 3], right[3]]), "lat", 1)
     down = from_behind(jnp.stack([left[0], kv[0, 0], kv[1, 0], right[0]]), "lat", -1)
-    q = jnp.dot(grouped, w_qkv[:, :WIDTH], preferred_element_type=jnp.float32)
-    q = q.astype(jnp.bfloat16).reshape(shape + (WIDTH,))
-    meta, tables = bias_inputs(bias_table, index_table, pad_mask, lax.axis_index("lat"), lat_total)
+    before = from_behind(bias_table[-1], "lat", 1)
+    lat_index = lax.axis_index("lat").astype(jnp.int32).reshape(1)
+    in_vmem = pl.BlockSpec(memory_space=pltpu.VMEM)
+    in_smem = pl.BlockSpec(memory_space=pltpu.SMEM)
+    highs = -(-bias_table.shape[-1] // LOW)
     bias = pl.pallas_call(
         bias_kernel,
-        out_shape=jax.ShapeDtypeStruct((2, 2, 3, 72, 8, 256), jnp.float32),
-        in_specs=[pl.BlockSpec(memory_space=pltpu.VMEM)] * 2,
-        out_specs=pl.BlockSpec(memory_space=pltpu.VMEM),
+        out_shape=jax.ShapeDtypeStruct((2, 2, 3, 36, 16, 256), jnp.bfloat16),
+        in_specs=[in_vmem] * 3 + [in_smem] * 2 + [in_vmem] * 5,
+        out_specs=in_vmem,
+        scratch_shapes=[
+            pltpu.VMEM((WIN_TOK + 32, 128), jnp.int32),
+            pltpu.VMEM((WIN_TOK + 32, 128), jnp.int32),
+            pltpu.VMEM((2, highs * 48, LOW), jnp.bfloat16),
+        ],
         compiler_params=pltpu.CompilerParams(vmem_limit_bytes=24 << 20),
         cost_estimate=pl.CostEstimate(
             flops=2 * 82 * 624 * 256 * 256, bytes_accessed=8 << 20, transcendentals=0
         ),
         name="bias",
-    )(meta, tables)
-    vectors = jnp.stack([proj_bias, norm_gain, norm_shift])
+    )(index_table, before, bias_table, pad_mask, lat_index, *bias_constants())
+    vectors = [v.reshape(1, features) for v in (proj_bias, norm_gain, norm_shift)]
     whole = pl.BlockSpec(memory_space=pltpu.VMEM)
 
     def bias_block(i):
@@ -352,7 +417,7 @@
         attend_kernel,
         grid=(8,),
         out_shape=jax.ShapeDtypeStruct((levels * lat_rows, lon_columns, features), jnp.bfloat16),
-        in_specs=[pl.BlockSpec((1, 1, 3, GROUP, 8, 256), bias_block)] + [whole] * 10,
+        in_specs=[pl.BlockSpec((1, 1, 3, GROUP // 2, 16, 256), bias_block)] + [whole] * 11,
         out_specs=whole,
         scratch_shapes=[
             pltpu.VMEM((6, 2, WIN_TOK, 2 * WIDTH), jnp.bfloat16),
@@ -362,7 +427,7 @@
             vmem_limit_bytes=40 << 20, dimension_semantics=("arbitrary",)
         ),
         name="attend",
-    )(bias, q, kv, left, right, up, down, hidden, restore, w_proj, vectors)
+    )(bias, qkv, left, right, up, down, hidden, restore, w_proj, *vectors)
     return out.reshape(state_tokens.shape)
 
 

time: 130 us -> 81.9 us (0.63)
  other arithmetic: 37.6 us -> 3.13 us
  local copies, waits for them, and re-layouts: 40.3 us -> 9.26 us
  waiting for transfers between devices: 0.01 us -> 20.3 us
  matrix products: 7.88 us -> 4.04 us
  Pallas kernels: 35.1 us -> 37.1 us
    convert_element_type x4 -> x0, other arithmetic: 30.2 us -> none  [allowed_pairs(): rows.append(((usable == 1) & same_row & same_level).astype(jnp.int32))]
    ppermute x5, waiting for transfers between devices: 0.01 us -> 20.3 us  [from_behind(): lax.ppermute(shard, axis, [(i, (i + by) % size) for i in range(size)])]
    another operation x12 -> x0, local copies, waits for them, and re-layouts: 12.1 us -> none  [the longest x7 7.01 us: bias_inputs(): meta = jnp.stack([as_tiles(r) for r in rows], axis=1)]
    reshape x12 -> x3, local copies, waits for them, and re-layouts: 7.48 us -> 0.01 us  [on_device(): v.reshape(1, features)]
    slice x27 -> x0, local copies, waits for them, and re-layouts: 6.99 us -> none  [the longest x3 3.12 us: kinds(): return jnp.stack([table[0, :8], table[1, :8], last])]
    unnamed x89 -> x46, local copies, waits for them, and re-layouts: 4.98 us -> 1.05 us
    dot_general x5 -> x1, matrix products: 7.88 us -> 4.04 us  [on_device(): qkv = jnp.dot(grouped, w_qkv, preferred_element_type=jnp.float32)]
    another operation x7 -> x0, other arithmetic: 3.46 us -> none  [the longest x3 2.67 us: bias_inputs(): tables = jnp.stack([jnp.stack([third, second]), jnp.stack([first, second])])]
  transfers between devices with their start and end apart: 5 -> 5, of which waited for: 0 -> 1; matrix products, arithmetic and copies ran while one was open for 60% -> 5% of each run, Pallas kernels for 16% -> 27%
where the time goes in v2:
time: 81.9 us; the launch traced here: 80.9 us
  Pallas kernels  37.1 us (45%)
  waiting for transfers between devices  20.3 us (25%)
  local copies, waits for them, and re-layouts  9.26 us (11%)
  starting transfers between devices  6.68 us (8%)
  matrix products  4.04 us (5%)
  other arithmetic  3.13 us (4%)
    pallas_call x1, Pallas kernels, on_device(): pl.pallas_call(bias_kernel, out_shape=jax.ShapeDtypeStruct((2, 2, 3, 36,...  22.1 us
    ppermute x5, waiting for transfers between devices, from_behind(): lax.ppermute(shard, axis, [(i, (i + by) % size) for i in range(size)])  20.3 us
    pallas_call x1, Pallas kernels, on_device(): pl.pallas_call(attend_kernel, grid=(8,), out_shape=jax.ShapeDtypeStruct((...  15 us
    ppermute x5, starting transfers between devices, from_behind(): lax.ppermute(shard, axis, [(i, (i + by) % size) for i in range(size)])  6.68 us
    dot_general x1, matrix products, on_device(): qkv = jnp.dot(grouped, w_qkv, preferred_element_type=jnp.float32)  4.04 us
  transfers between devices with their start and end apart: 5, of which 1 were waited for; matrix products, arithmetic and copies ran while one was open for 5% of the time, Pallas kernels for 27%

profile of v2, /device:TPU:0, one launch (start us, length us, event | category | flops | bytes accessed | tf_op | source)
XLA Modules:
  0.0 80.9 jit_solution(6533350264573457748)
XLA Ops:
  0.0 0.8 %broadcast_compare_fusion = pred[12,12]{1,0:T(8,128)(4,1)S(1)} fusion(s32[12,12]{1,0:T(8,128)} %param.19), kind=kLoop, calls=%fused_computation.18 | loop fusion | flops 144 | bytes 720 | tf_op jit(solution)/shard_map/eq | solution.py:370
  0.8 0.8 slice_reduce_fusion.1
  1.6 0.1 broadcast_select_fusion
  1.7 1.6 %add_convert_fusion = bf16[4,12,12,768]{3,0,2,1:T(4,128)(2,1)S(1)} fusion(bf16[4,12,12,768]{3,0,2,1:T(4,128)(2,1)} %param.18, f32[12,12,768]{2,1,0:T(8,128)S(1)} %broadcast_select_fusion), kind=kLoop, calls=%fused_computation.5 | loop fusion | flops 1327104 | bytes 2211840 | tf_op jit(solution)/shard_map/convert_element_type | solution.py:371
  3.4 0.0 copy-start.21
  3.4 0.1 copy.23
  3.5 1.2 %pad.4.clone = bf16[4,12,16,768]{3,2,1,0:T(8,128)(2,1)} pad(bf16[4,12,12,768]{3,2,1,0:T(8,128)(2,1)S(1)} %copy.23, bf16[]{:T(256)} %constant.22.clone.1), padding=0_0x0_0x0_4x0_0 | pad | bytes 2064386 | tf_op jit(solution)/shard_map/jit(_pad)/pad | solution.py:372
  4.7 0.0 copy-done
  4.7 4.0 %convolution_convert_fusion = bf16[768,1152]{1,0:T(8,128)(2,1)S(1)} fusion(bf16[768,1152]{1,0:T(8,128)(2,1)S(1)} %copy-done, bf16[768,768]{1,0:T(8,128)(2,1)} %bitcast.23, s32[768]{0:T(1024)S(1)} %copy-done.21), kind=kOutput, calls=%fused_computation | convolution fusion | flops 2266988544 | bytes 4721664 | tf_op jit(solution)/shard_map/dot_general | solution.py:381
  8.7 0.0 copy-start.16
  8.8 1.1 %slice_bitcast_fusion = (bf16[4,2,48,768]{3,2,1,0:T(8,128)(2,1)}, bf16[4,2,48,768]{3,2,1,0:T(8,128)(2,1)}) fusion(bf16[2,4,2,48,1152]{4,3,2,1,0:T(8,128)(2,1)S(1)} %bitcast.20), kind=kLoop, calls=%fused_computation.8 | loop fusion | bytes 2359296 | tf_op jit(solution)/shard_map/squeeze | solution.py:384
  9.9 6.1 %collective-permute-start.2 = (bf16[4,2,48,768]{3,2,1,0:T(8,128)(2,1)}, bf16[4,2,48,768]{3,2,1,0:T(8,128)(2,1)}, u32[]{:S(2)}, u32[]{:S(2)}) collective-permute-start(bf16[4,2,48,768]{3,2,1,0:T(8,128)(2,1)} %get-tuple-element.11), channel_id=1, source_target_pairs={{0,14},{2,0},{4,2},{6,4},{8,6},{10,8},{12,10},{14,12},{1,15},{3,1}... | collective-permute-start | bytes 1769480 | tf_op jit(solution)/shard_map/ppermute | solution.py:28
  16.0 0.7 slice_bitcast_fusion.2
  16.7 0.8 copy-done.2
  17.4 0.0 collective-permute-start
  17.4 0.0 collective-permute-start.1
  17.5 0.8 %slice_bitcast_fusion.4 = (bf16[1,2,48,768]{3,2,1,0:T(8,128)(2,1)}, bf16[1,2,48,768]{3,2,1,0:T(8,128)(2,1)}, bf16[1,2,48,768]{3,2,1,0:T(8,128)(2,1)}, bf16[1,2,48,768]{3,2,1,0:T(8,128)(2,1)}) fusion(bf16[2,4,2,48,1152]{4,3,2,1,0:T(8,128)(2,1)S(1)} %bitcast.21), kind=kLoop, calls=%fused_computation.15 | loop fusion | bytes 1179648 | tf_op jit(solution)/shard_map/stack;squeeze | solution.py:387
  18.3 0.0 copy-done.19
  18.4 0.4 fusion.1.restore_ref
  18.8 0.0 copy-start.5
  18.8 0.0 copy-start.6
  18.8 0.0 copy-start.7
  18.8 0.0 copy-start.8
  18.9 0.0 copy-start.9
  18.9 0.0 copy-start.10
  18.9 0.0 copy-start.11
  18.9 20.3 %collective-permute-done.2.right_ref = bf16[4,2,48,768]{3,2,1,0:T(8,128)(2,1)} collective-permute-done((bf16[4,2,48,768]{3,2,1,0:T(8,128)(2,1)}, bf16[4,2,48,768]{3,2,1,0:T(8,128)(2,1)}, u32[]{:S(2)}, u32[]{:S(2)}) %collective-permute-start.2) | collective-permute-done | bytes 589856 | tf_op jit(solution)/shard_map/ppermute | solution.py:28
  39.2 1.0 %fusion.5 = (bf16[1,2,48,768]{3,2,1,0:T(8,128)(2,1)S(1)}, bf16[1,2,48,768]{3,2,1,0:T(8,128)(2,1)S(1)}) fusion(bf16[4,2,48,768]{3,2,1,0:T(8,128)(2,1)} %collective-permute-done.2.right_ref), kind=kLoop, calls=%fused_computation.22 | loop fusion | bytes 589824 | tf_op jit(solution)/shard_map/slice | solution.py:387
  40.2 0.0 collective-permute-done.1.left_ref
  40.2 1.0 %fusion.4 = (bf16[1,2,48,768]{3,2,1,0:T(8,128)(2,1)S(1)}, bf16[1,2,48,768]{3,2,1,0:T(8,128)(2,1)S(1)}) fusion(bf16[4,2,48,768]{3,2,1,0:T(8,128)(2,1)} %collective-permute-done.1.left_ref), kind=kLoop, calls=%fused_computation.21 | loop fusion | bytes 589824 | tf_op jit(solution)/shard_map/slice | solution.py:387
  41.2 0.1 pad_maximum_fusion
  41.3 0.1 collective-permute-start.3
  41.4 0.1 pad_maximum_fusion.1
  41.5 0.5 collective-permute-start.4
  42.0 0.0 collective-permute-done.before_ref
  42.0 0.0 copy-done.5
  42.0 0.0 copy-done.6
  42.1 0.0 copy-done.7
  42.1 0.0 copy-done.8
  42.1 0.0 copy-done.9
  42.1 0.0 copy-done.10
  42.1 0.0 copy-done.11
  42.1 0.0 copy-start.4
  42.1 22.1 %bias.1.bias_ref = bf16[2,2,3,36,16,256]{5,4,3,2,1,0:T(8,128)(2,1)S(1)} custom-call(s32[144,144]{1,0:T(8,128)S(1)} %copy-done.5, bf16[2,12,3312]{2,1,0:T(8,128)(2,1)} %collective-permute-done.before_ref, bf16[2,2,12,3312]{3,2,1,0:T(8,128)(2,1)S(1)} %copy-done.3, s32[24]{0:T(128)S(1)} %copy-done.6, s32[1]{0:T(128)} %bitcast.1.lat_ref, ...), custom_call_target="tpu_custom_call" | custom-call | flops 6706692096 | bytes 8388608 | tf_op jit(solution)/shard_map/bias/pallas_call | solution.py:393
  64.3 0.0 collective-permute-done.3.up_ref
  64.3 0.0 collective-permute-done.4.down_ref
  64.3 15.0 %attend.1 = bf16[48,12,768]{2,1,0:T(8,128)(2,1)S(1)} custom-call(bf16[2,2,3,36,16,256]{5,4,3,2,1,0:T(8,128)(2,1)S(1)} %bias.1.bias_ref, bf16[2,4,2,48,1152]{4,3,2,1,0:T(8,128)(2,1)S(1)} %bitcast.22, bf16[4,2,48,768]{3,2,1,0:T(8,128)(2,1)} %collective-permute-done.1.left_ref, bf16[4,2,48,768]{3,2,1,0:T(8,128)(2,1)} %collective-permute-done.2.right_ref, ...), custom_call_target="tpu_custom_call" | custom-call | tf_op jit(solution)/shard_map/attend/pallas_call | solution.py:416
  79.3 1.6 %copy.22 = bf16[4,12,12,768]{3,0,2,1:T(4,128)(2,1)} copy(bf16[4,12,12,768]{3,2,1,0:T(8,128)(2,1)S(1)} %bitcast.25) | data formatting | bytes 1769472 | tf_op jit(solution)/shard_map/reshape | solution.py:431
  (28 shorter events, 0.1 us)
Async XLA Ops:
  0.0 4.7 %copy-start = (bf16[768,1152]{1,0:T(8,128)(2,1)S(1)}, bf16[768,1152]{1,0:T(8,128)(2,1)}, u32[]{:S(2)}) copy-start(bf16[768,1152]{1,0:T(8,128)(2,1)} %param.22) | copy-start | bytes 5308420
  3.4 1.3 %copy-start.21 = (s32[768]{0:T(1024)S(1)}, s32[768]{0:T(1024)}, u32[]{:S(2)}) copy-start(s32[768]{0:T(1024)} %constant.23.clone) | copy-start | bytes 9220
  8.7 7.2 %copy-start.16 = (bf16[2,2,12,3312]{3,1,2,0:T(2,128)(2,1)S(1)}, bf16[2,2,12,3312]{3,1,2,0:T(2,128)(2,1)}, u32[]{:S(2)}) copy-start(bf16[2,2,12,3312]{3,1,2,0:T(2,128)(2,1)} %param.27) | copy-start | bytes 953860
  9.9 8.4 %copy-start.18 = (f32[768]{0:T(1024)S(1)}, f32[768]{0:T(1024)}, u32[]{:S(2)}) copy-start(f32[768]{0:T(1024)} %param.24) | copy-start | bytes 9220
  9.9 8.4 %copy-start.19 = (f32[768]{0:T(1024)S(1)}, f32[768]{0:T(1024)}, u32[]{:S(2)}) copy-start(f32[768]{0:T(1024)} %param.25) | copy-start | bytes 9220
  9.9 8.5 %copy-start.20 = (f32[768]{0:T(1024)S(1)}, f32[768]{0:T(1024)}, u32[]{:S(2)}) copy-start(f32[768]{0:T(1024)} %param.26) | copy-start | bytes 9220
  9.9 8.5 %copy-start.17 = (s32[768]{0:T(1024)S(1)}, s32[768]{0:T(1024)}, u32[]{:S(2)}) copy-start(s32[768]{0:T(1024)} %constant.24.clone) | copy-start | bytes 9220
  9.9 29.3 %collective-permute-start.2 = (bf16[4,2,48,768]{3,2,1,0:T(8,128)(2,1)}, bf16[4,2,48,768]{3,2,1,0:T(8,128)(2,1)}, u32[]{:S(2)}, u32[]{:S(2)}) collective-permute-start(bf16[4,2,48,768]{3,2,1,0:T(8,128)(2,1)} %get-tuple-element.11), channel_id=1, source_target_pairs={{0,14},{2,0},{4,2},{6,4},{8,6},{10,8},{12,10},{14,12},{1,15},{3,1}... | collective-permute-start | bytes 1769480 | tf_op jit(solution)/shard_map/ppermute | solution.py:28
  16.7 0.8 copy-start.2
  17.4 24.6 %collective-permute-start = (bf16[2,12,3312]{2,1,0:T(8,128)(2,1)}, bf16[2,12,3312]{2,1,0:T(8,128)(2,1)}, u32[]{:S(2)}, u32[]{:S(2)}) collective-permute-start(bf16[2,12,3312]{2,1,0:T(8,128)(2,1)} %slice_bitcast_fusion.2), channel_id=1, source_target_pairs={{0,1},{1,0},{2,3},{3,2},{4,5},{5,4},{6,7},{7,6},{8,9},{9,8},{10,11... | collective-permute-start | bytes 476936 | tf_op jit(solution)/shard_map/ppermute | solution.py:28
  17.4 22.7 %collective-permute-start.1 = (bf16[4,2,48,768]{3,2,1,0:T(8,128)(2,1)}, bf16[4,2,48,768]{3,2,1,0:T(8,128)(2,1)}, u32[]{:S(2)}, u32[]{:S(2)}) collective-permute-start(bf16[4,2,48,768]{3,2,1,0:T(8,128)(2,1)} %get-tuple-element.12), channel_id=1, source_target_pairs={{0,2},{2,4},{4,6},{6,8},{8,10},{10,12},{12,14},{14,0},{1,3},{3,5},... | collective-permute-start | bytes 1769480 | tf_op jit(solution)/shard_map/ppermute | solution.py:28
  18.3 22.9 %copy-start.14 = (bf16[1,2,48,768]{3,2,1,0:T(8,128)(2,1)S(1)}, bf16[1,2,48,768]{3,2,1,0:T(8,128)(2,1)}, u32[]{:S(2)}) copy-start(bf16[1,2,48,768]{3,2,1,0:T(8,128)(2,1)} %get-tuple-element.9) | copy-start | bytes 442372
  18.3 22.9 %copy-start.15 = (bf16[1,2,48,768]{3,2,1,0:T(8,128)(2,1)S(1)}, bf16[1,2,48,768]{3,2,1,0:T(8,128)(2,1)}, u32[]{:S(2)}) copy-start(bf16[1,2,48,768]{3,2,1,0:T(8,128)(2,1)} %get-tuple-element.10) | copy-start | bytes 442372
  18.4 23.0 %copy-start.12 = (bf16[1,2,48,768]{3,2,1,0:T(8,128)(2,1)S(1)}, bf16[1,2,48,768]{3,2,1,0:T(8,128)(2,1)}, u32[]{:S(2)}) copy-start(bf16[1,2,48,768]{3,2,1,0:T(8,128)(2,1)} %get-tuple-element.7) | copy-start | bytes 442372
  18.4 23.0 %copy-start.13 = (bf16[1,2,48,768]{3,2,1,0:T(8,128)(2,1)S(1)}, bf16[1,2,48,768]{3,2,1,0:T(8,128)(2,1)}, u32[]{:S(2)}) copy-start(bf16[1,2,48,768]{3,2,1,0:T(8,128)(2,1)} %get-tuple-element.8) | copy-start | bytes 442372
  18.8 23.2 %copy-start.3 = (bf16[2,2,12,3312]{3,2,1,0:T(8,128)(2,1)S(1)}, bf16[2,2,12,3312]{3,2,1,0:T(8,128)(2,1)}, u32[]{:S(2)}) copy-start(bf16[2,2,12,3312]{3,2,1,0:T(8,128)(2,1)} %copy-done.2) | copy-start | bytes 953860
  18.8 23.2 %copy-start.5 = (s32[144,144]{1,0:T(8,128)S(1)}, s32[144,144]{1,0:T(8,128)}, u32[]{:S(2)}) copy-start(s32[144,144]{1,0:T(8,128)} %index_ref.1) | copy-start | bytes 248836
  18.8 23.2 %copy-start.6 = (s32[24]{0:T(128)S(1)}, s32[24]{0:T(128)}, u32[]{:S(2)}) copy-start(s32[24]{0:T(128)} %pad_ref.1) | copy-start | bytes 292
  18.8 23.2 %copy-start.7 = (s32[82,3,256]{2,1,0:T(4,128)S(1)}, s32[82,3,256]{2,1,0:T(4,128)}, u32[]{:S(2)}) copy-start(s32[82,3,256]{2,1,0:T(4,128)} %constant.29.clone.geometry_ref) | copy-start | bytes 755716
  18.8 23.2 %copy-start.8 = (bf16[160,144]{1,0:T(8,128)(2,1)S(1)}, bf16[160,144]{1,0:T(8,128)(2,1)}, u32[]{:S(2)}) copy-start(bf16[160,144]{1,0:T(8,128)(2,1)} %constant.27.clone.to_q_rest_ref) | copy-start | bytes 138244
  18.9 23.2 %copy-start.9 = (bf16[144,256]{1,0:T(8,128)(2,1)S(1)}, bf16[144,256]{1,0:T(8,128)(2,1)}, u32[]{:S(2)}) copy-start(bf16[144,256]{1,0:T(8,128)(2,1)} %constant.28.clone.to_k_rest_ref) | copy-start | bytes 221188
  18.9 23.2 %copy-start.10 = (bf16[144,144]{1,0:T(8,128)(2,1)S(1)}, bf16[144,144]{1,0:T(8,128)(2,1)}, u32[]{:S(2)}) copy-start(bf16[144,144]{1,0:T(8,128)(2,1)} %constant.25.clone.to_q_ref) | copy-start | bytes 124420
  18.9 23.2 %copy-start.11 = (bf16[144,128]{1,0:T(8,128)(2,1)S(1)}, bf16[144,128]{1,0:T(8,128)(2,1)}, u32[]{:S(2)}) copy-start(bf16[144,128]{1,0:T(8,128)(2,1)} %constant.26.clone.to_k_ref) | copy-start | bytes 110596
  41.3 22.9 %collective-permute-start.3 = (bf16[4,2,48,768]{3,2,1,0:T(8,128)(2,1)S(1)}, bf16[4,2,48,768]{3,2,1,0:T(8,128)(2,1)S(1)}, u32[]{:S(2)}, u32[]{:S(2)}) collective-permute-start(bf16[4,2,48,768]{3,2,1,0:T(8,128)(2,1)S(1)} %pad_maximum_fusion), channel_id=1, source_target_pairs={{0,1},{1,0},{2,3},{3,2},{4,5},{5,4},{6,7},{7,6},{8,9},{9,8},{10,11... | collective-permute-start | bytes 1769480 | tf_op jit(solution)/shard_map/ppermute | solution.py:28
  41.5 22.8 %collective-permute-start.4 = (bf16[4,2,48,768]{3,2,1,0:T(8,128)(2,1)S(1)}, bf16[4,2,48,768]{3,2,1,0:T(8,128)(2,1)S(1)}, u32[]{:S(2)}, u32[]{:S(2)}) collective-permute-start(bf16[4,2,48,768]{3,2,1,0:T(8,128)(2,1)S(1)} %pad_maximum_fusion.1), channel_id=1, source_target_pairs={{0,1},{1,0},{2,3},{3,2},{4,5},{5,4},{6,7},{7,6},{8,9},{9,8},{10,11... | collective-permute-start | bytes 1769480 | tf_op jit(solution)/shard_map/ppermute | solution.py:28
  42.1 22.2 %copy-start.1 = (bf16[4,12,16,768]{3,2,1,0:T(8,128)(2,1)S(1)}, bf16[4,12,16,768]{3,2,1,0:T(8,128)(2,1)}, u32[]{:S(2)}) copy-start(bf16[4,12,16,768]{3,2,1,0:T(8,128)(2,1)} %pad.4.clone) | copy-start | bytes 3538948
  42.1 22.2 %copy-start.4 = (bf16[384,768]{1,0:T(8,128)(2,1)S(1)}, bf16[384,768]{1,0:T(8,128)(2,1)}, u32[]{:S(2)}) copy-start(bf16[384,768]{1,0:T(8,128)(2,1)} %w_ref.1) | copy-start | bytes 1769476
